TPU v7x, 128 devices: a whole 4x4x4 slice. The times are simulated.
128 devices in a mesh: tok: 8 (over z_lo, x), row: 4 (over z_hi, core), col: 4 (over y).
Axes of the slice: x: 4, y: 4, z: 4 (z_hi: 2, z_lo: 2; z = z_hi * 2 + z_lo), core: 2. Of those that a mesh axis runs over, the one named last changes fastest.
Arguments:
- activations: bfloat16 [2, 1024, 28672], P(None, 'tok', ('row', 'col')), may hold values from -0.1875 to 0.1875
- weights: bfloat16 [2, 28672, 8192], P(None, ('row', 'col'), 'tok'), may hold values from -6 to 6
Outputs:
- solved: float32 [256, 8192], P('row', ('tok', 'col'))
- correction: bfloat16 [28672, 8192], P(('row', 'col'), 'tok')
All inputs are finite; a program needn't handle non-finite values.
Results may differ from a plain program's by a relative error of at most 0.0073.
Values may be sent and summed in bfloat16 or wider, within the bound.
A program may use at most 64 MiB of HBM per device.

v0:
```python
import jax
import jax.numpy as jnp
from jax import lax
from jax.sharding import PartitionSpec as P

PANEL = 256


def broadcast(array, axis, root):
    return lax.dynamic_index_in_dim(lax.all_gather(array, axis), root, 0, keepdims=False)


def in_blocks(array, dim, peers):
    lengths = array.shape
    tiles = array.reshape(*lengths[:dim], peers, lengths[dim] // peers, *lengths[dim + 1 :])
    return jnp.moveaxis(tiles, dim, 0)


def summed_on_arrival(array, axis, dim):
    peers = lax.axis_size(axis)
    tiles = lax.all_to_all(in_blocks(array, dim, peers), axis, 0, 0, tiled=True)
    return jnp.sum(tiles, axis=0)


def joined_along(tiles, dim):
    tiles = jnp.moveaxis(tiles, 0, dim)
    lengths = tiles.shape
    return tiles.reshape(*lengths[:dim], lengths[dim] * lengths[dim + 1], *lengths[dim + 2 :])


def from_everyone(array, axis):
    peers = lax.axis_size(axis)
    return lax.all_to_all(
        jnp.broadcast_to(array[None], (peers, *array.shape)), axis, 0, 0, tiled=True
    )


def gather_directly(array, axis, dim):
    return joined_along(from_everyone(array, axis), dim)


def body(activations, weights):
    row_count = lax.axis_size("row")
    col_count = lax.axis_size("col")
    rows_here = activations.shape[2]
    panel_width = PANEL
    block_rows = panel_width // row_count
    out_here = weights.shape[2]
    block_cols = out_here // col_count
    first_row = lax.axis_index(("row", "col")) * rows_here
    panel_tokens = broadcast(activations[:, :, :panel_width], ("row", "col"), 0)
    partial_value = jnp.einsum(
        "mti,mtp->mip", activations, panel_tokens, preferred_element_type=jnp.float32
    )
    gram_sums = lax.psum(partial_value, "tok")
    row_ids = first_row + jnp.arange(rows_here, dtype=jnp.int32)[:, None]
    col_ids = jnp.arange(panel_width, dtype=jnp.int32)[None, :]
    on_diagonal = row_ids == col_ids
    regular = gram_sums * jnp.where(on_diagonal, 1.0, 0.9).astype(jnp.float32)[None]
    regular_bf16 = regular.astype(jnp.bfloat16)
    summed = regular[0] + regular[1]
    offset = jnp.int32(0)
    outputs = []
    for position in range(block_rows * lax.axis_size(("row", "col")) // block_rows):
        block_id = offset // block_rows + position
        tile_row = block_id // col_count
        tile_col = block_id % col_count
        gram_part = lax.dynamic_slice_in_dim(regular_bf16, tile_row * block_rows, block_rows, 2)
        weight_part = lax.dynamic_slice_in_dim(weights, tile_col * block_cols, block_cols, 2)
        outputs.append(
            jnp.einsum("mip,mio->po", gram_part, weight_part, preferred_element_type=jnp.float32)
        )
    right_block = summed_on_arrival(jnp.concatenate(outputs, axis=0), ("row", "col"), 0)
    diagonal_part = broadcast(summed[:panel_width], ("row", "col"), 0)
    factor = jnp.linalg.cholesky(diagonal_part)
    panel_factor = lax.linalg.triangular_solve(
        factor, summed, left_side=False, lower=True, transpose_a=True
    )
    row_index = lax.axis_index("row")
    whole_right = gather_directly(right_block, "row", 0)
    whole_solved = lax.linalg.triangular_solve(factor, whole_right, left_side=True, lower=True)
    solved = lax.dynamic_slice_in_dim(whole_solved, row_index * block_rows, block_rows, 0)
    solved_columns = lax.all_gather(solved, "col", axis=1, tiled=True)
    correction = jnp.dot(
        panel_factor,
        lax.all_gather(solved_columns, "row", axis=0, tiled=True),
        precision=lax.Precision.HIGHEST,
        preferred_element_type=jnp.float32,
    )
    return (solved, correction.astype(jnp.bfloat16))


def solution(mesh):
    in_specs = (P(None, "tok", ("row", "col")), P(None, ("row", "col"), "tok"))
    out_specs = (P("row", ("tok", "col")), P(("row", "col"), "tok"))
    return jax.shard_map(body, mesh=mesh, in_specs=in_specs, out_specs=out_specs, check_vma=False)
```

profile of v0, /device:TPU:1, one launch (start us, length us, event | category | flops | bytes accessed | tf_op | source)
XLA Modules:
  0.0 338.8 jit_solution(6505781074480112813)
XLA Ops:
  7.2 0.0 all-gather.9.cloned.1.call-start
  7.2 1.6 slice.77
  8.8 0.0 all-reduce.3.cloned.1.call-start
  8.9 54.1 %all-gather.9.cloned.1.call-done = bf16[32,128,256]{2,1,0:T(8,128)(2,1)} async-done(((bf16[2,128,256]{2,1,0:T(8,128)(2,1)}), bf16[32,128,256]{2,1,0:T(8,128)(2,1)}) %all-gather.9.cloned.1.call-update) | async-done | bytes 2097168 | tf_op jit(solution)/shard_map/all_gather | solution.py:10
  62.9 3.7 %fusion.151 = f32[2,1792,256]{2,1,0:T(8,128)} fusion(bf16[2,128,1792]{2,1,0:T(8,128)(2,1)} %param.2, bf16[32,128,256]{2,1,0:T(8,128)(2,1)} %all-gather.9.cloned.1.call-done), kind=kOutput, calls=%fused_computation.101 | convolution fusion | flops 234881024 | bytes 4718592 | tf_op jit(solution)/shard_map/mti,mtp->mip/dot_general | solution.py:52
  66.6 0.0 all-reduce.3.cloned.1.call-update
  66.6 0.0 all-gather.5.cloned.1.call-start
  66.7 0.3 fusion.3
  67.0 94.8 %all-reduce.3.cloned.1.call-done = f32[2,1792,256]{2,1,0:T(8,128)} async-done(((f32[2,1792,256]{2,1,0:T(8,128)}), f32[2,1792,256]{2,1,0:T(8,128)}) %all-reduce.3.cloned.1.call-update) | async-done | bytes 3670032 | tf_op jit(solution)/shard_map/psum | solution.py:55
  161.8 3.8 %fusion.163 = (bf16[2,1792,256]{2,1,0:T(8,128)(2,1)}, f32[2,1792,256]{2,1,0:T(8,128)S(1)}) fusion(f32[2,1792,256]{2,1,0:T(8,128)} %all-reduce.3.cloned.1.call-done, f32[1792,256]{1,0:T(8,128)S(1)} %fusion.3), kind=kLoop, calls=%fused_computation.126 | loop fusion | flops 1835008 | bytes 11010048 | tf_op jit(solution)/shard_map/convert_element_type | solution.py:60
  165.6 0.2 slice_add_fusion
  165.8 1.6 copy-done
  167.5 0.7 slice.96
  168.2 0.0 all-gather.5.cloned.1.call-update
  168.2 0.2 copy-done.1
  168.4 2.1 fusion.39
  170.5 2.0 fusion.63
  172.5 2.1 fusion.87
  174.6 2.0 fusion.111
  176.6 2.3 fusion.45
  179.0 0.8 fusion.69
  179.7 0.8 fusion.93
  180.5 0.8 fusion.117
  181.3 0.5 fusion.51
  181.8 0.5 fusion.75
  182.3 0.5 fusion.99
  182.8 0.5 fusion.123
  183.3 0.8 fusion.57
  184.0 0.8 fusion.81
  184.8 0.8 fusion.105
  185.6 0.8 fusion.129
  186.3 25.9 %all_to_all.10 = f32[16,64,256]{2,1,0:T(8,128)S(1)} all-to-all(f32[16,64,256]{2,1,0:T(8,128)S(1)} %bitcast.111), channel_id=1, replica_groups=mesh['tok'=8,'row'=4,'col'=4] {'row','col'}, dimensions={0} | all-to-all | bytes 2097152 | tf_op jit(solution)/shard_map/all_to_all | solution.py:21
  212.2 0.1 reduce_sum.9
  212.3 0.7 broadcast_in_dim.21
  213.0 5.3 %all-to-all-start.1 = ((f32[4,64,256]{2,1,0:T(8,128)}), f32[4,64,256]{2,1,0:T(8,128)S(1)}, u32[]{:S(2)}, u32[]{:S(2)}) async-start(f32[4,64,256]{2,1,0:T(8,128)} %broadcast_in_dim.21), calls=%async_computation.1 | async-start | bytes 524288 | tf_op jit(solution)/shard_map/all_to_all | solution.py:33
  218.3 6.5 %all-to-all-done.1 = f32[4,64,256]{2,1,0:T(8,128)S(1)} async-done(((f32[4,64,256]{2,1,0:T(8,128)}), f32[4,64,256]{2,1,0:T(8,128)S(1)}, u32[]{:S(2)}, u32[]{:S(2)}) %all-to-all-start.1) | async-done | bytes 262176 | tf_op jit(solution)/shard_map/all_to_all | solution.py:33
  224.9 5.5 %all-gather.5.cloned.1.call-done = f32[16,256,256]{2,1,0:T(8,128)} async-done(((f32[1,256,256]{2,1,0:T(8,128)}), f32[16,256,256]{2,1,0:T(8,128)}) %all-gather.5.cloned.1.call-update) | async-done | bytes 4194320 | tf_op jit(solution)/shard_map/all_gather | solution.py:10
  230.4 1.0 dynamic_slice.70
  231.3 0.1 copy.43
  231.5 1.0 fusion.150
  232.5 11.7 %cholesky.50 = f32[128,128]{1,0:T(8,128)S(1)} custom-call(f32[128,128]{1,0:T(8,128)S(1)} %cholesky.118), custom_call_target="Cholesky" | custom-call | tf_op jit(solution)/shard_map/jit(cholesky)/cholesky | solution.py:75
  244.2 9.8 %custom-call.16 = f32[1,128,128]{1,2,0:T(8,128)S(1)} custom-call(f32[1,128,128]{2,1,0:T(8,128)S(1)} %get-tuple-element.27), custom_call_target="InvertDiagBlocksLowerTriangular" | custom-call | tf_op jit(solution)/shard_map/jit(cholesky)/cholesky | solution.py:75
  254.0 0.2 constant_dynamic-update-slice_fusion
  254.3 0.3 convolution_subtract_fusion.2
  254.5 11.7 %cholesky.105 = f32[128,128]{1,0:T(8,128)S(1)} custom-call(f32[128,128]{1,0:T(8,128)S(1)} %convolution_subtract_fusion.2), custom_call_target="Cholesky" | custom-call | tf_op jit(solution)/shard_map/jit(cholesky)/cholesky | solution.py:75
  266.3 0.7 compare_reduce_fusion
  268.3 0.1 triangular_solve.76
  268.4 4.2 %while.1 = (s32[]{:T(128)}, f32[256,256]{1,0:T(8,128)S(1)}, s32[2,2]{1,0:T(2,128)S(1)}, f32[2,128,128]{2,1,0:T(8,128)S(1)}, s32[]{:T(128)}) while((s32[]{:T(128)}, f32[256,256]{1,0:T(8,128)S(1)}, s32[2,2]{1,0:T(2,128)S(1)}, f32[2,128,128]{2,1,0:T(8,128)S(1)}, s32[]{:T(128)}) %tuple.29), condition=%wide.while_cond, body=%wide.while_body.sunk | while | flops 2 | bytes 131181 | solution.py:81
  268.5 0.6 fusion.177
  269.2 1.3 bitcast_dynamic-update-slice_fusion.2
  270.6 0.6 fusion.177
  271.2 1.3 bitcast_dynamic-update-slice_fusion.2
  272.6 19.7 %custom-call.17 = f32[2,128,128]{1,2,0:T(8,128)S(1)} custom-call(f32[2,128,128]{2,1,0:T(8,128)S(1)} %get-tuple-element.9), custom_call_target="InvertDiagBlocksLowerTriangular" | custom-call | tf_op jit(solution)/shard_map/triangular_solve | solution.py:81
  292.3 0.3 fusion.157
  292.6 0.3 convolution_subtract_fusion.1
  292.9 0.3 fusion.159
  293.2 10.1 %all_gather.19 = f32[64,1024]{1,0:T(8,128)} all-gather(f32[64,256]{1,0:T(8,128)S(1)} %fusion.153), channel_id=1, replica_groups=mesh['tok'=8,'row'=4,'col'=4] {'col'}, dimensions={1}, use_global_device_ids=true | all-gather | bytes 327680 | tf_op jit(solution)/shard_map/all_gather | solution.py:83
  303.3 0.0 all-gather.7.cloned.1.call-update
  303.4 2.3 fusion.175
  305.7 1.0 fusion.132
  306.6 1.6 convolution_subtract_fusion
  308.2 1.0 fusion.158
  309.2 14.3 %all-gather.7.cloned.1.call-done = f32[256,1024]{1,0:T(8,128)} async-done(((f32[64,1024]{1,0:T(8,128)}), f32[256,1024]{1,0:T(8,128)}) %all-gather.7.cloned.1.call-update) | async-done | bytes 1048592 | tf_op jit(solution)/shard_map/all_gather | solution.py:86
  323.5 8.7 %convolution_convert_fusion = bf16[1792,1024]{1,0:T(8,128)(2,1)} fusion(f32[256,1024]{1,0:T(8,128)} %all-gather.7.cloned.1.call-done, f32[1792,128]{0,1:T(8,128)S(1)} %fusion.158, f32[1792,128]{0,1:T(8,128)S(1)} %fusion.132), kind=kOutput, calls=%fused_computation.2 | convolution fusion | flops 5639438336 | bytes 6553600 | tf_op jit(solution)/shard_map/dot_general | solution.py:84
  (23 shorter events, 0.2 us)
Async XLA Ops:
  7.2 55.7 %all-gather.9.cloned.1.call-start = ((), (), s32[]{:S(2)}) async-start(), calls=%async_computation.5 | async-start | bytes 2228224 | tf_op jit(solution)/shard_map/all_gather | solution.py:10
  8.8 153.0 %all-reduce.3.cloned.1.call-start = ((), (), s32[]{:S(2)}) async-start(), calls=%async_computation.2 | async-start | bytes 7340032 | tf_op jit(solution)/shard_map/psum | solution.py:55
  66.6 163.7 %all-gather.5.cloned.1.call-start = ((), (), s32[]{:S(2)}) async-start(), calls=%async_computation.3 | async-start | bytes 4456448 | tf_op jit(solution)/shard_map/all_gather | solution.py:10
  165.6 1.9 copy-start
  165.6 2.8 copy-start.1
  168.4 10.5 %slice-start = ((s8[7340032]{0:T(1024)(128)(4,1)}), s8[4194304]{0:T(1024)(128)(4,1)S(1)}, s32[]{:S(2)}) async-start(s8[7340032]{0:T(1024)(128)(4,1)} %bitcast.114), calls=%async_computation.6 | async-start | bytes 8388608
  172.5 6.5 %slice-start.1 = ((s8[7340032]{0:T(1024)(128)(4,1)}), s8[3145728]{0:T(1024)(128)(4,1)S(1)}, s32[]{:S(2)}) async-start(s8[7340032]{0:T(1024)(128)(4,1)} %bitcast.114), calls=%async_computation.7 | async-start | bytes 6291456
  213.0 11.8 %all-to-all-start.1 = ((f32[4,64,256]{2,1,0:T(8,128)}), f32[4,64,256]{2,1,0:T(8,128)S(1)}, u32[]{:S(2)}, u32[]{:S(2)}) async-start(f32[4,64,256]{2,1,0:T(8,128)} %broadcast_in_dim.21), calls=%async_computation.1 | async-start | bytes 524288 | tf_op jit(solution)/shard_map/all_to_all | solution.py:33
  218.3 105.2 %all-gather.7.cloned.1.call-start = ((), (), s32[]{:S(2)}) async-start(), calls=%async_computation.4 | async-start | bytes 1310720 | tf_op jit(solution)/shard_map/all_gather | solution.py:86
  293.2 12.4 %copy-start.2 = (f32[64,256]{1,0:T(8,128)}, f32[64,256]{1,0:T(8,128)S(1)}, u32[]{:S(2)}) copy-start(f32[64,256]{1,0:T(8,128)S(1)} %fusion.153) | copy-start | bytes 196612
Sparse Core Ops, SparseCore 0:
  11.0 51.8 all-gather.8
  66.8 95.0 all-reduce.2
  168.3 61.9 all-gather.4
  303.5 20.0 all-gather.6
where the time goes:
time: 339 us
  waiting for transfers between devices  175 us (52%)
  other arithmetic  61.4 us (18%)
  blocking collectives  36 us (11%)
  matrix products  35.1 us (10%)
  between operations  15.3 us (5%)
  local copies, waits for them, and re-layouts  10.1 us (3%)
  starting transfers between devices  5.42 us (2%)
    psum x1, waiting for transfers between devices, body(): gram_sums = lax.psum(partial_value, 'tok')  94.8 us
    all_gather x2, waiting for transfers between devices, broadcast(): lax.all_gather(array, axis)  59.5 us
    another operation x6, other arithmetic, body(): factor = jnp.linalg.cholesky(diagonal_part)  34 us
    all_to_all x1, blocking collectives, summed_on_arrival(): tiles = lax.all_to_all(in_blocks(array, dim, peers), axis, 0, 0, tiled=True)  25.9 us
    another operation x4, other arithmetic, body(): lax.linalg.triangular_solve(factor, whole_right, left_side=True, lower=True)  19.7 us
    dot_general x16, matrix products, body(): jnp.einsum('mip,mio->po', gram_part, weight_part, preferred_element_type=...  17.8 us
    all_gather x1, waiting for transfers between devices, body(): lax.all_gather(solved_columns, 'row', axis=0, tiled=True)  14.3 us
    all_gather x1, blocking collectives, body(): solved_columns = lax.all_gather(solved, 'col', axis=1, tiled=True)  10.1 us
  transfers between devices with their start and end apart: 5, of which 5 were waited for; matrix products, arithmetic and copies ran while one was open for 7% of the time, Pallas kernels for 0%

commit v1 on v0

v1 whole, which is shorter than its diff:
```python
import jax
import jax.numpy as jnp
from jax import lax
from jax.experimental import pallas as pl
from jax.experimental.pallas import tpu as pltpu
from jax.sharding import PartitionSpec as P

PANEL = 256
STEP = 16
MESH = pl.DeviceIdType.MESH
HIGHEST = lax.Precision.HIGHEST
F32 = jnp.float32
BF16 = jnp.bfloat16


def split3(value):
    high = value.astype(BF16)
    rest = value - high.astype(F32)
    middle = rest.astype(BF16)
    low = (rest - middle.astype(F32)).astype(BF16)
    return high, middle, low


def eliminate(step, big):
    base = pl.multiple_of(step * STEP, STEP)
    per_half = 128 // STEP
    rows = [big[h, pl.ds(base, STEP), :] for h in range(4)]
    shift = lax.rem(128 - lax.rem(step, per_half) * STEP, 128)
    diag = pltpu.roll(big[step // per_half, pl.ds(base, STEP), :], shift, 1)
    cols = [jnp.broadcast_to(diag[:, j : j + 1], (STEP, 128)) for j in range(STEP)]
    ids = lax.broadcasted_iota(jnp.int32, (STEP, 128), 0)
    for p in range(STEP):
        inverse = lax.rsqrt(cols[p][p : p + 1, :])
        lcol = cols[p] * inverse
        below = jnp.where(ids > p, lcol, 0.0)
        for h in range(4):
            pivot = rows[h][p : p + 1, :] * inverse
            rows[h] = jnp.where(ids == p, pivot, rows[h] - below * pivot)
        for j in range(p + 1, STEP):
            cols[j] = cols[j] - lcol * lcol[j : j + 1, :]
    for h in range(4):
        big[h, pl.ds(base, STEP), :] = rows[h]
    wide = jnp.concatenate(rows, axis=1)
    lane = lax.broadcasted_iota(jnp.int32, (STEP, PANEL), 1)
    left = jnp.where(lane >= base + STEP, wide[:, :PANEL], 0.0)
    lh, lm, ll = split3(left)
    rh, rm, rl = split3(wide)
    lhs = jnp.concatenate([lh, lh, lm, lm, lh, ll], axis=0)
    rhs = jnp.concatenate([rh, rm, rh, rm, rl, rh], axis=0)
    update = lax.dot_general(
        lhs, rhs, (((0,), (0,)), ((), ())), preferred_element_type=F32
    )
    for h in range(4):
        big[h] = big[h] - update[:, 128 * h : 128 * h + 128]


def first_unit(t, core):
    return 7 * (t // 2) + lax.rem(t, 2) * (4 - core)


def has_fourth(t, core):
    return lax.rem(t + core, 2) == 0


def kernel(
    acts, wts, zout, smout, solout,
    xv, wv, pb, pt, xg, gt, rp, rsend, rin, r2, r2in, zb, solb, solin, big, sinv,
    xsem, wsem, p1send, p2send, p3send, precv, xsend, xrecv, gsend, grecv,
    dsend, drecv, rsems, rrecv, zsend, zfwd, zrecv, ssend, srecv,
):
    t = lax.axis_index("tok")
    row = lax.axis_index("row")
    col = lax.axis_index("col")
    core = lax.rem(row, 2)
    zhi = row // 2
    partner = {"row": row + 1 - 2 * core}

    def remote(src, dst, ss, rs, dev):
        return pltpu.make_async_remote_copy(
            src_ref=src, dst_ref=dst, send_sem=ss, recv_sem=rs, device_id=dev,
            device_id_type=MESH,
        )

    def arrived(ref, sem):
        pltpu.make_async_copy(ref, ref, sem).wait()

    load_x = pltpu.make_async_copy(acts, xv, xsem)
    load_x.start()
    load_w = pltpu.make_async_copy(wts, wv, wsem)
    load_w.start()

    barrier = pltpu.get_barrier_semaphore()
    for d in range(1, 8):
        pl.semaphore_signal(
            barrier, inc=1, device_id={"tok": lax.rem(t + d, 8)}, device_id_type=MESH
        )
    for e in range(1, 16):
        dev = {"row": lax.rem(row + e // 4, 4), "col": lax.rem(col + e % 4, 4)}
        pl.semaphore_signal(barrier, inc=1, device_id=dev, device_id_type=MESH)
    load_x.wait()
    pl.semaphore_wait(barrier, 22)

    source = jnp.logical_and(row == 0, col == 0)

    def p1(e):
        m = (e // 4) % 2
        return remote(
            xv.at[m, :, 0:PANEL], pb.at[m, t], p1send.at[e], precv.at[m, t],
            {"row": e // 4, "col": e % 4},
        )

    @pl.when(source)
    def _():
        pltpu.make_async_copy(acts.at[0, :, 0:PANEL], pb.at[0, t], precv.at[0, t]).start()
        for e in range(1, 16):
            p1(e).start()

    def xcopy(d, slot):
        tt = lax.rem(t + d, 8)
        unit = first_unit(tt, core) + slot
        lanes = pl.ds(pl.multiple_of(lax.rem(unit, 14) * 128, 128), 128)
        if d == 0:
            return pltpu.make_async_copy(
                acts.at[unit // 14, :, lanes], xg.at[slot, t], xrecv.at[slot]
            )
        return remote(
            xv.at[unit // 14, :, lanes], xg.at[slot, t], xsend.at[slot * 8 + d],
            xrecv.at[slot], {"tok": tt},
        )

    def send_slot(slot):
        for d in range(8):
            if slot < 3:
                xcopy(d, slot).start()
            else:
                @pl.when(has_fourth(lax.rem(t + d, 8), core))
                def _():
                    xcopy(d, slot).start()

    send_slot(0)

    def p2(d):
        return remote(
            pb.at[core, t], pb.at[core, t], p2send.at[d], precv.at[core, t],
            {"tok": lax.rem(t + d, 8)},
        )

    def p3(d):
        tt = lax.rem(t + d, 8)
        return remote(
            pb.at[core, tt], pb.at[core, tt], p3send.at[d], precv.at[core, tt], partner
        )

    arrived(pb.at[core, t], precv.at[core, t])
    for d in range(1, 8):
        p2(d).start()
    p3(0).start()
    for slot in range(1, 4):
        send_slot(slot)
    for d in range(1, 8):
        tt = lax.rem(t + d, 8)
        arrived(pb.at[core, tt], precv.at[core, tt])
        p3(d).start()
    for d in range(8):
        tt = lax.rem(t + d, 8)
        arrived(pb.at[1 - core, tt], precv.at[1 - core, tt])

    total = jnp.zeros((PANEL, PANEL), F32)
    for m in range(2):
        tokens = pb[m].reshape(1024, PANEL)
        flipped = jnp.transpose(tokens)
        pt[m] = flipped
        total = total + jnp.dot(flipped, tokens, preferred_element_type=F32)
    ii = lax.broadcasted_iota(jnp.int32, (PANEL, 128), 0)
    jj = lax.broadcasted_iota(jnp.int32, (PANEL, 128), 1)
    for h in range(2):
        on = ii == jj + 128 * h
        big[h] = total[:, 128 * h : 128 * h + 128] * jnp.where(on, 1.0, 0.9)
        big[2 + h] = jnp.where(on, 1.0, 0.0)

    def panels(first, last):
        def one(step, carry):
            eliminate(step, big)
            return carry

        lax.fori_loop(first, last, one, 0)

    panels(0, 5)

    own = first_unit(t, core)

    def gcopy(slot, d):
        return remote(
            gt.at[own + slot], gt.at[own + slot], gsend.at[slot * 8 + d],
            grecv.at[own + slot], {"tok": lax.rem(t + d, 8)},
        )

    def gram(slot):
        arrived(xg.at[slot], xrecv.at[slot])
        unit = own + slot
        first = (row * 4 + col) * 1792 + lax.rem(unit, 14) * 128
        product = jnp.dot(
            pt[unit // 14], xg[slot].reshape(1024, 128), preferred_element_type=F32
        )
        gt[unit] = (product * jnp.where(ii == jj + first, 1.0, 0.9)).astype(BF16)
        for d in range(1, 8):
            gcopy(slot, d).start()

    for slot in range(3):
        gram(slot)

    @pl.when(has_fourth(t, core))
    def _():
        gram(3)

    panels(5, 16)
    inverse = jnp.concatenate([big[2], big[3]], axis=1)
    sinv[...] = lax.dot_general(
        inverse, inverse, (((0,), (0,)), ((), ())), precision=HIGHEST,
        preferred_element_type=F32,
    )

    load_w.wait()
    count = jnp.where(has_fourth(t, core), 4, 3)

    def accumulate(i, carry):
        for k in range(2):
            unit = 2 * i + k

            @pl.when(jnp.logical_or(unit < own, unit >= own + count))
            def _():
                arrived(gt.at[unit], grecv.at[unit])

        lhs = jnp.concatenate([gt[2 * i], gt[2 * i + 1]], axis=1)
        feats = pl.ds(pl.multiple_of(lax.rem(i, 7) * 256, 256), 256)
        part = jnp.dot(lhs, wv[i // 7, feats, :], preferred_element_type=F32)
        for q in range(8):
            piece = part[:, 128 * q : 128 * q + 128]
            rp[q] = jnp.where(i == 0, piece, rp[q] + piece)
        return carry

    lax.fori_loop(0, 14, accumulate, 0)

    def flip(first, last):
        for j in range(first, last):
            both = gt[j].astype(F32) + gt[14 + j].astype(F32)
            smout[128 * j : 128 * j + 128, :] = jnp.transpose(both).astype(BF16)

    def group(i, which):
        return 2 * i + lax.rem(which + i, 2)

    def dcopy(i):
        return remote(rsend.at[i], rin.at[i], dsend.at[i], drecv.at[i], partner)

    for i in range(4):
        rsend[i] = rp[group(i, 1 - core)].astype(BF16)
        dcopy(i).start()
    flip(0, 5)
    solver = lax.rem(col + zhi, 2) == core
    chip = zhi * 4 + col
    mine = 2 * col + zhi

    def mine_is(i):
        return jnp.logical_and(solver, i == col)

    def rcopy(i):
        dev = {"row": 2 * lax.rem(core + i, 2) + core, "col": i}
        return remote(r2.at[i], r2in.at[chip], rsems.at[i], rrecv.at[chip], dev)

    for i in range(4):
        arrived(rin.at[i], drecv.at[i])
        r2[i] = (rp[group(i, core)] + rin[i].astype(F32)).astype(BF16)

        @pl.when(jnp.logical_not(mine_is(i)))
        def _():
            rcopy(i).start()

    flip(5, 10)

    def zcopy(e):
        dev = {
            "row": 2 * lax.rem(zhi + e // 4, 2) + core, "col": lax.rem(col + e % 4, 4)
        }
        return remote(zb.at[mine], zb.at[mine], zsend.at[e], zrecv.at[mine], dev)

    def scopy(rr):
        return remote(
            solb.at[pl.ds(64 * rr, 64), :], solin.at[zhi], ssend.at[rr], srecv.at[zhi],
            {"row": rr, "col": col},
        )

    @pl.when(solver)
    def _():
        whole = rp[mine] + rin[col].astype(F32)
        for e in range(1, 8):
            other = lax.rem(chip + e, 8)
            arrived(r2in.at[other], rrecv.at[other])
            whole = whole + r2in[other].astype(F32)
        answer = jnp.dot(sinv[...], whole, precision=HIGHEST, preferred_element_type=F32)
        zb[mine] = answer.astype(BF16)
        for e in range(1, 8):
            zcopy(e).start()
        inverse = jnp.concatenate([big[2], big[3]], axis=1)
        solb[...] = jnp.dot(inverse, whole, precision=HIGHEST, preferred_element_type=F32)
        for rr in range(4):
            @pl.when(rr != row)
            def _():
                scopy(rr).start()

            @pl.when(rr == row)
            def _():
                solin[zhi] = solb[64 * rr : 64 * rr + 64, :]

    flip(10, 14)

    def zforward(i):
        q = group(i, core)
        return remote(zb.at[q], zb.at[q], zfwd.at[i], zrecv.at[q], partner)

    for i in range(4):
        q = group(i, core)

        @pl.when(jnp.logical_not(mine_is(i)))
        def _():
            arrived(zb.at[q], zrecv.at[q])

        zforward(i).start()
    for i in range(4):
        q = group(i, 1 - core)
        arrived(zb.at[q], zrecv.at[q])
    for q in range(8):
        zout[:, 128 * q : 128 * q + 128] = zb[q]
    for h in range(2):
        @pl.when(jnp.logical_not(jnp.logical_and(solver, zhi == h)))
        def _():
            arrived(solin.at[h], srecv.at[h])

        solout[:, 128 * h : 128 * h + 128] = solin[h]

    @pl.when(source)
    def _():
        for e in range(1, 16):
            p1(e).wait_send()

    for d in range(8):
        p3(d).wait_send()
    for d in range(1, 8):
        p2(d).wait_send()
        for slot in range(3):
            xcopy(d, slot).wait_send()
            gcopy(slot, d).wait_send()

        @pl.when(has_fourth(lax.rem(t + d, 8), core))
        def _():
            xcopy(d, 3).wait_send()

        @pl.when(has_fourth(t, core))
        def _():
            gcopy(3, d).wait_send()

    for i in range(4):
        dcopy(i).wait_send()
        zforward(i).wait_send()

        @pl.when(jnp.logical_not(mine_is(i)))
        def _():
            rcopy(i).wait_send()

    @pl.when(solver)
    def _():
        for e in range(1, 8):
            zcopy(e).wait_send()
        for rr in range(4):
            @pl.when(rr != row)
            def _():
                scopy(rr).wait_send()


def body(activations, weights):
    dma = pltpu.SemaphoreType.DMA
    vmem = pltpu.VMEM
    outs = pl.pallas_call(
        kernel,
        out_shape=(
            jax.ShapeDtypeStruct((256, 1024), BF16),
            jax.ShapeDtypeStruct((1792, 256), BF16),
            jax.ShapeDtypeStruct((64, 256), F32),
        ),
        in_specs=[pl.BlockSpec(memory_space=pl.ANY)] * 2,
        out_specs=(pl.BlockSpec(memory_space=pltpu.VMEM),) * 3,
        scratch_shapes=[
            vmem((2, 128, 1792), BF16), vmem((2, 1792, 1024), BF16),
            vmem((2, 8, 128, 256), BF16), vmem((2, 256, 1024), BF16),
            vmem((4, 8, 128, 128), BF16), vmem((28, 256, 128), BF16),
            vmem((8, 256, 128), F32), vmem((4, 256, 128), BF16),
            vmem((4, 256, 128), BF16), vmem((4, 256, 128), BF16),
            vmem((8, 256, 128), BF16), vmem((8, 256, 128), BF16),
            vmem((256, 128), F32), vmem((2, 64, 128), F32),
            vmem((4, 256, 128), F32), vmem((256, 256), F32),
            dma, dma, dma((16,)), dma((8,)), dma((8,)), dma((2, 8)), dma((32,)),
            dma((4,)), dma((32,)), dma((28,)), dma((4,)), dma((4,)), dma((4,)),
            dma((8,)), dma((8,)), dma((4,)), dma((8,)), dma((4,)), dma((2,)),
        ],
        compiler_params=pltpu.CompilerParams(
            collective_id=0, has_side_effects=True, vmem_limit_bytes=48 * 1024 * 1024
        ),
    )(activations, weights)
    answer, grams, solved = outs
    correction = jnp.dot(grams, answer, preferred_element_type=F32)
    return solved, correction.astype(BF16)


def solution(mesh):
    in_specs = (P(None, "tok", ("row", "col")), P(None, ("row", "col"), "tok"))
    out_specs = (P("row", ("tok", "col")), P(("row", "col"), "tok"))
    return jax.shard_map(
        body, mesh=mesh, in_specs=in_specs, out_specs=out_specs, check_vma=False
    )
```

time: 339 us -> 80.1 us (0.24)
  waiting for transfers between devices: 175 us -> 0 us
  Pallas kernels: 0 us -> 74.6 us
  other arithmetic: 61.4 us -> 0 us
  blocking collectives: 36 us -> 0 us
  matrix products: 35.1 us -> 2.95 us
  between operations: 15.3 us -> 0.65 us
  local copies, waits for them, and re-layouts: 10.1 us -> 1.8 us
  starting transfers between devices: 5.42 us -> 0 us
    psum x1 -> x0, waiting for transfers between devices: 94.8 us -> none  [body(): gram_sums = lax.psum(partial_value, 'tok')]
    pallas_call x0 -> x1, Pallas kernels: none -> 74.6 us  [body(): pl.pallas_call(kernel, out_shape=(jax.ShapeDtypeStruct((256, 1024), BF16)...]
    all_gather x3 -> x0, waiting for transfers between devices: 73.9 us -> none  [the longest x2 59.5 us: broadcast(): lax.all_gather(array, axis)]
    another operation x10 -> x0, other arithmetic: 53.7 us -> none  [the longest x6 34 us: body(): factor = jnp.linalg.cholesky(diagonal_part)]
    dot_general x18 -> x1, matrix products: 30.2 us -> 2.95 us  [body(): correction = jnp.dot(grams, answer, preferred_element_type=F32)]
    all_to_all x1 -> x0, blocking collectives: 25.9 us -> none  [summed_on_arrival(): tiles = lax.all_to_all(in_blocks(array, dim, peers), axis, 0, 0, tiled=True)]
    all_gather x1 -> x0, blocking collectives: 10.1 us -> none  [body(): solved_columns = lax.all_gather(solved, 'col', axis=1, tiled=True)]
    all_to_all x1 -> x0, waiting for transfers between devices: 6.54 us -> none  [from_everyone(): lax.all_to_all(jnp.broadcast_to(array[None], (peers, *array.shape)), axis...]
  transfers between devices with their start and end apart: 5 -> 0, of which waited for: 5 -> 0; matrix products, arithmetic and copies ran while one was open for 7% -> 0% of each run, Pallas kernels for 0% -> 0%
where the time goes in v1:
time: 80.1 us; the launch traced here: 80 us
  Pallas kernels  74.6 us (93%)
  matrix products  2.95 us (4%)
  local copies, waits for them, and re-layouts  1.8 us (2%)
    pallas_call x1, Pallas kernels, body(): pl.pallas_call(kernel, out_shape=(jax.ShapeDtypeStruct((256, 1024), BF16)...  74.6 us
    dot_general x1, matrix products, body(): correction = jnp.dot(grams, answer, preferred_element_type=F32)  2.95 us
    unnamed x3, local copies, waits for them, and re-layouts  1.8 us

profile of v1, /device:TPU:1, one launch (start us, length us, event | category | flops | bytes accessed | tf_op | source)
XLA Modules:
  0.0 80.0 jit_solution(1722933435733229538)
XLA Ops:
  0.6 0.0 copy-start
  0.6 1.2 %copy-done = bf16[2,128,1792]{2,1,0:T(8,128)(2,1)S(1)} copy-done((bf16[2,128,1792]{2,1,0:T(8,128)(2,1)S(1)}, bf16[2,128,1792]{2,1,0:T(8,128)(2,1)}, u32[]{:S(2)}) %copy-start) | copy-done | bytes 917528
  1.8 74.6 %shard_map.41 = (bf16[256,1024]{1,0:T(8,128)(2,1)S(1)}, bf16[1792,256]{1,0:T(8,128)(2,1)S(1)}, f32[64,256]{1,0:T(8,128)S(1)}) custom-call(bf16[2,128,1792]{2,1,0:T(8,128)(2,1)S(1)} %copy-done, bf16[2,1792,1024]{2,1,0:T(8,128)(2,1)} %wts.1), custom_call_target="tpu_custom_call" | custom-call | tf_op jit(solution)/shard_map/pallas_call | solution.py:382
  76.4 3.0 %convolution_convert_fusion = bf16[1792,1024]{1,0:T(8,128)(2,1)} fusion(bf16[1792,256]{1,0:T(8,128)(2,1)S(1)} %get-tuple-element.6, bf16[256,1024]{1,0:T(8,128)(2,1)S(1)} %get-tuple-element.7), kind=kOutput, calls=%fused_computation | convolution fusion | flops 941359104 | bytes 5111808 | tf_op jit(solution)/shard_map/dot_general | solution.py:409
  79.3 0.6 copy.5
Async XLA Ops:
  0.6 1.2 %copy-start = (bf16[2,128,1792]{2,1,0:T(8,128)(2,1)S(1)}, bf16[2,128,1792]{2,1,0:T(8,128)(2,1)}, u32[]{:S(2)}) copy-start(bf16[2,128,1792]{2,1,0:T(8,128)(2,1)} %acts.1) | copy-start | bytes 2752516

commit v2 on v1

--- a/solution.py
+++ b/solution.py
@@ -64,8 +64,9 @@
 
 def kernel(
     acts, wts, zout, smout, solout,
-    xv, wv, pb, pt, xg, gt, rp, rsend, rin, r2, r2in, zb, solb, solin, big, sinv,
-    xsem, wsem, p1send, p2send, p3send, precv, xsend, xrecv, gsend, grecv,
+    xv, wv, pa, pb, pt, xg, gt, rp, rsend, rin, r2, r2in, zb, solb, solin, big, sinv,
+    xsem, wsem, asend, arecv, bsend, brecv, csend, crecv, fsend, frecv,
+    xsend, xrecv, gsend, grecv, hsend,
     dsend, drecv, rsems, rrecv, zsend, zfwd, zrecv, ssend, srecv,
 ):
     t = lax.axis_index("tok")
@@ -73,7 +74,12 @@
     col = lax.axis_index("col")
     core = lax.rem(row, 2)
     zhi = row // 2
+    zlo = t // 4
+    x = lax.rem(t, 4)
     partner = {"row": row + 1 - 2 * core}
+
+    def at(dx, dz):
+        return lax.rem(zlo + dz, 2) * 4 + lax.rem(x + dx, 4)
 
     def remote(src, dst, ss, rs, dev):
         return pltpu.make_async_remote_copy(
@@ -86,8 +92,12 @@
 
     load_x = pltpu.make_async_copy(acts, xv, xsem)
     load_x.start()
-    load_w = pltpu.make_async_copy(wts, wv, wsem)
-    load_w.start()
+    load_w = [
+        pltpu.make_async_copy(wts.at[m], wv.at[pl.ds(1792 * m, 1792), :], wsem.at[m])
+        for m in range(2)
+    ]
+    for load in load_w:
+        load.start()
 
     barrier = pltpu.get_barrier_semaphore()
     for d in range(1, 8):
@@ -97,29 +107,35 @@
     for e in range(1, 16):
         dev = {"row": lax.rem(row + e // 4, 4), "col": lax.rem(col + e % 4, 4)}
         pl.semaphore_signal(barrier, inc=1, device_id=dev, device_id_type=MESH)
+
+    wv[3584:, :] = jnp.zeros((128, 1024), BF16)
+    for k in range(4):
+        gt[2 * k + 1 - core, 3] = jnp.zeros((PANEL, 128), BF16)
     load_x.wait()
     pl.semaphore_wait(barrier, 22)
 
     source = jnp.logical_and(row == 0, col == 0)
 
-    def p1(e):
-        m = (e // 4) % 2
+    def scatter(e):
+        first = 16 * (e // 4 % 2 * 4 + e % 4)
         return remote(
-            xv.at[m, :, 0:PANEL], pb.at[m, t], p1send.at[e], precv.at[m, t],
+            xv.at[:, first : first + 16, 0:PANEL], pa, asend.at[e], arecv,
             {"row": e // 4, "col": e % 4},
         )
 
     @pl.when(source)
     def _():
-        pltpu.make_async_copy(acts.at[0, :, 0:PANEL], pb.at[0, t], precv.at[0, t]).start()
-        for e in range(1, 16):
-            p1(e).start()
+        for e in (4, 1, 3, 5, 7, 8, 9, 11, 12, 13, 15, 2, 6, 10, 14):
+            scatter(e).start()
+        pa[...] = xv[:, 0:16, 0:PANEL]
+
+    offsets = ((1, 1), (3, 0), (0, 1), (3, 1), (1, 0), (2, 1), (2, 0))
 
     def xcopy(d, slot):
-        tt = lax.rem(t + d, 8)
+        tt = t if d == 7 else at(*offsets[d])
         unit = first_unit(tt, core) + slot
         lanes = pl.ds(pl.multiple_of(lax.rem(unit, 14) * 128, 128), 128)
-        if d == 0:
+        if d == 7:
             return pltpu.make_async_copy(
                 acts.at[unit // 14, :, lanes], xg.at[slot, t], xrecv.at[slot]
             )
@@ -133,46 +149,110 @@
             if slot < 3:
                 xcopy(d, slot).start()
             else:
-                @pl.when(has_fourth(lax.rem(t + d, 8), core))
+                tt = t if d == 7 else at(*offsets[d])
+
+                @pl.when(has_fourth(tt, core))
                 def _():
                     xcopy(d, slot).start()
 
     send_slot(0)
 
-    def p2(d):
+    def spread(d):
         return remote(
-            pb.at[core, t], pb.at[core, t], p2send.at[d], precv.at[core, t],
-            {"tok": lax.rem(t + d, 8)},
-        )
-
-    def p3(d):
-        tt = lax.rem(t + d, 8)
-        return remote(
-            pb.at[core, tt], pb.at[core, tt], p3send.at[d], precv.at[core, tt], partner
-        )
-
-    arrived(pb.at[core, t], precv.at[core, t])
-    for d in range(1, 8):
-        p2(d).start()
-    p3(0).start()
+            pa, pb.at[:, t, core, col], bsend.at[d], brecv, {"tok": at(*offsets[d])}
+        )
+
+    @pl.when(jnp.logical_not(source))
+    def _():
+        arrived(pa, arecv)
+
+    for d in range(7):
+        spread(d).start()
+    pb[:, t, core, col] = pa[...]
     for slot in range(1, 4):
         send_slot(slot)
-    for d in range(1, 8):
-        tt = lax.rem(t + d, 8)
-        arrived(pb.at[core, tt], precv.at[core, tt])
-        p3(d).start()
-    for d in range(8):
-        tt = lax.rem(t + d, 8)
-        arrived(pb.at[1 - core, tt], precv.at[1 - core, tt])
-
-    total = jnp.zeros((PANEL, PANEL), F32)
-    for m in range(2):
-        tokens = pb[m].reshape(1024, PANEL)
-        flipped = jnp.transpose(tokens)
-        pt[m] = flipped
-        total = total + jnp.dot(flipped, tokens, preferred_element_type=F32)
+    arrived(pb.at[:, 0:7, core, col], brecv)
+
+    def along(k, d):
+        m = lax.rem(zlo + k, 2)
+        piece = pb.at[m, :, core, col]
+        return remote(
+            piece, piece, csend.at[k * 4 + d], crecv.at[k, col],
+            {"col": lax.rem(col + d, 4)},
+        )
+
+    def across(k, d):
+        m = lax.rem(zlo + k, 2)
+        piece = pb.at[m, :, core, lax.rem(col + d, 4)]
+        return remote(piece, piece, fsend.at[k * 4 + d], frecv.at[k], partner)
+
+    for k in range(2):
+        for d in (1, 3, 2):
+            along(k, d).start()
+    for k in range(2):
+        across(k, 0).start()
+
+    def collect(k):
+        m = lax.rem(zlo + k, 2)
+        for d in (1, 3, 2):
+            other = lax.rem(col + d, 4)
+            arrived(pb.at[m, :, core, other], crecv.at[k, other])
+            across(k, d).start()
+
+    def whole_panel(k):
+        m = lax.rem(zlo + k, 2)
+        arrived(pb.at[m, :, 1 - core], frecv.at[k])
+        return pb[m].reshape(1024, PANEL)
+
+    collect(0)
+    tokens = whole_panel(0)
+    flipped = jnp.transpose(tokens)
+    pt[...] = flipped
+
     ii = lax.broadcasted_iota(jnp.int32, (PANEL, 128), 0)
     jj = lax.broadcasted_iota(jnp.int32, (PANEL, 128), 1)
+    own = first_unit(t, core)
+    right, left, across_z, far = at(1, 0), at(3, 0), at(0, 1), at(2, 0)
+
+    def gcopy(tt, slot, to, sem):
+        return remote(
+            gt.at[tt, slot], gt.at[tt, slot], sem, grecv.at[tt, slot], {"tok": to}
+        )
+
+    def when_there(tt, slot, action):
+        if slot < 3:
+            action()
+        else:
+            pl.when(has_fourth(tt, core))(action)
+
+    def unit_in(tt, slot):
+        arrived(gt.at[tt, slot], grecv.at[tt, slot])
+
+    def own_sends(slot):
+        return [
+            gcopy(t, slot, to, gsend.at[slot * 3 + k])
+            for k, to in enumerate((right, left, across_z))
+        ]
+
+    def gram(slot):
+        arrived(xg.at[slot], xrecv.at[slot])
+        first = (row * 4 + col) * 1792 + lax.rem(own + slot, 14) * 128
+        product = jnp.dot(
+            pt[...], xg[slot].reshape(1024, 128), preferred_element_type=F32
+        )
+        gt[t, slot] = (product * jnp.where(ii == jj + first, 1.0, 0.9)).astype(BF16)
+        for copy in own_sends(slot):
+            copy.start()
+
+    for slot in range(4):
+        when_there(t, slot, lambda slot=slot: gram(slot))
+
+    total = jnp.dot(pt[...], pb[zlo].reshape(1024, PANEL), preferred_element_type=F32)
+    collect(1)
+    tokens = whole_panel(1)
+    total = total + lax.dot_general(
+        tokens, tokens, (((0,), (0,)), ((), ())), preferred_element_type=F32
+    )
     for h in range(2):
         on = ii == jj + 128 * h
         big[h] = total[:, 128 * h : 128 * h + 128] * jnp.where(on, 1.0, 0.9)
@@ -185,66 +265,93 @@
 
         lax.fori_loop(first, last, one, 0)
 
-    panels(0, 5)
-
-    own = first_unit(t, core)
-
-    def gcopy(slot, d):
-        return remote(
-            gt.at[own + slot], gt.at[own + slot], gsend.at[slot * 8 + d],
-            grecv.at[own + slot], {"tok": lax.rem(t + d, 8)},
-        )
-
-    def gram(slot):
-        arrived(xg.at[slot], xrecv.at[slot])
-        unit = own + slot
-        first = (row * 4 + col) * 1792 + lax.rem(unit, 14) * 128
-        product = jnp.dot(
-            pt[unit // 14], xg[slot].reshape(1024, 128), preferred_element_type=F32
-        )
-        gt[unit] = (product * jnp.where(ii == jj + first, 1.0, 0.9)).astype(BF16)
-        for d in range(1, 8):
-            gcopy(slot, d).start()
-
-    for slot in range(3):
-        gram(slot)
-
-    @pl.when(has_fourth(t, core))
-    def _():
-        gram(3)
-
-    panels(5, 16)
+    def accumulate(tt, start=False):
+        lhs = jnp.concatenate([gt[tt, slot] for slot in range(4)], axis=1)
+        feats = pl.ds(pl.multiple_of(first_unit(tt, core) * 128, 128), 512)
+        part = jnp.dot(lhs, wv[feats, :], preferred_element_type=F32)
+        for q in range(8):
+            piece = part[:, 128 * q : 128 * q + 128]
+            rp[q] = piece if start else rp[q] + piece
+
+    def relay_z(slot):
+        return [
+            gcopy(across_z, slot, to, hsend.at[slot * 2 + k])
+            for k, to in enumerate((right, left))
+        ]
+
+    def relay_x(slot):
+        if slot < 2:
+            return left, gcopy(left, slot, right, hsend.at[8 + slot])
+        return right, gcopy(right, slot, left, hsend.at[8 + slot])
+
+    def relay_far(slot):
+        return gcopy(far, slot, across_z, hsend.at[12 + slot])
+
+    def forward(slot):
+        def from_z():
+            unit_in(across_z, slot)
+            for copy in relay_z(slot):
+                copy.start()
+
+        def from_x():
+            tt, copy = relay_x(slot)
+            unit_in(tt, slot)
+            copy.start()
+
+        when_there(across_z, slot, from_z)
+        when_there(relay_x(slot)[0], slot, from_x)
+
+    def forward_far(slot):
+        def action():
+            unit_in(far, slot)
+            relay_far(slot).start()
+
+        when_there(far, slot, action)
+
+    def take(tt, slots=range(4)):
+        for slot in slots:
+            when_there(tt, slot, lambda slot=slot: unit_in(tt, slot))
+        accumulate(tt)
+
+    for load in load_w:
+        load.wait()
+    accumulate(t, True)
+    forward(0)
+    panels(0, 2)
+    forward(1)
+    panels(2, 4)
+    forward(2)
+    panels(4, 6)
+    forward(3)
+    accumulate(across_z)
+    forward_far(0)
+    panels(6, 8)
+    forward_far(1)
+    take(left, (2, 3))
+    forward_far(2)
+    panels(8, 10)
+    forward_far(3)
+    take(right, (0, 1))
+    panels(10, 13)
+    accumulate(far)
+    panels(13, 16)
     inverse = jnp.concatenate([big[2], big[3]], axis=1)
     sinv[...] = lax.dot_general(
         inverse, inverse, (((0,), (0,)), ((), ())), precision=HIGHEST,
         preferred_element_type=F32,
     )
-
-    load_w.wait()
-    count = jnp.where(has_fourth(t, core), 4, 3)
-
-    def accumulate(i, carry):
-        for k in range(2):
-            unit = 2 * i + k
-
-            @pl.when(jnp.logical_or(unit < own, unit >= own + count))
-            def _():
-                arrived(gt.at[unit], grecv.at[unit])
-
-        lhs = jnp.concatenate([gt[2 * i], gt[2 * i + 1]], axis=1)
-        feats = pl.ds(pl.multiple_of(lax.rem(i, 7) * 256, 256), 256)
-        part = jnp.dot(lhs, wv[i // 7, feats, :], preferred_element_type=F32)
-        for q in range(8):
-            piece = part[:, 128 * q : 128 * q + 128]
-            rp[q] = jnp.where(i == 0, piece, rp[q] + piece)
-        return carry
-
-    lax.fori_loop(0, 14, accumulate, 0)
-
-    def flip(first, last):
-        for j in range(first, last):
-            both = gt[j].astype(F32) + gt[14 + j].astype(F32)
-            smout[128 * j : 128 * j + 128, :] = jnp.transpose(both).astype(BF16)
+    take(at(1, 1))
+    take(at(3, 1))
+    take(at(2, 1))
+
+    def flip(c):
+        for slot in range(4):
+            def action(slot=slot):
+                both = gt[c, slot].astype(F32) + gt[c + 4, slot].astype(F32)
+                rows = pl.ds(pl.multiple_of((first_unit(c, core) + slot) * 128, 128), 128)
+                smout[rows, :] = jnp.transpose(both).astype(BF16)
+
+            when_there(c, slot, action)
 
     def group(i, which):
         return 2 * i + lax.rem(which + i, 2)
@@ -255,7 +362,7 @@
     for i in range(4):
         rsend[i] = rp[group(i, 1 - core)].astype(BF16)
         dcopy(i).start()
-    flip(0, 5)
+    flip(0)
     solver = lax.rem(col + zhi, 2) == core
     chip = zhi * 4 + col
     mine = 2 * col + zhi
@@ -275,7 +382,7 @@
         def _():
             rcopy(i).start()
 
-    flip(5, 10)
+    flip(1)
 
     def zcopy(e):
         dev = {
@@ -311,7 +418,8 @@
             def _():
                 solin[zhi] = solb[64 * rr : 64 * rr + 64, :]
 
-    flip(10, 14)
+    flip(2)
+    flip(3)
 
     def zforward(i):
         q = group(i, core)
@@ -340,23 +448,30 @@
     @pl.when(source)
     def _():
         for e in range(1, 16):
-            p1(e).wait_send()
-
-    for d in range(8):
-        p3(d).wait_send()
-    for d in range(1, 8):
-        p2(d).wait_send()
-        for slot in range(3):
-            xcopy(d, slot).wait_send()
-            gcopy(slot, d).wait_send()
-
-        @pl.when(has_fourth(lax.rem(t + d, 8), core))
-        def _():
-            xcopy(d, 3).wait_send()
-
-        @pl.when(has_fourth(t, core))
-        def _():
-            gcopy(3, d).wait_send()
+            scatter(e).wait_send()
+
+    for d in range(7):
+        spread(d).wait_send()
+        for slot in range(4):
+            when_there(
+                at(*offsets[d]), slot, lambda slot=slot: xcopy(d, slot).wait_send()
+            )
+    for k in range(2):
+        for d in range(4):
+            across(k, d).wait_send()
+            if d:
+                along(k, d).wait_send()
+    for slot in range(4):
+        def sent(slot=slot):
+            for copy in own_sends(slot):
+                copy.wait_send()
+            for copy in relay_z(slot):
+                copy.wait_send()
+            relay_far(slot).wait_send()
+
+        when_there(t, slot, sent)
+        tt, copy = relay_x(slot)
+        when_there(tt, slot, lambda copy=copy: copy.wait_send())
 
     for i in range(4):
         dcopy(i).wait_send()
@@ -389,16 +504,18 @@
         in_specs=[pl.BlockSpec(memory_space=pl.ANY)] * 2,
         out_specs=(pl.BlockSpec(memory_space=pltpu.VMEM),) * 3,
         scratch_shapes=[
-            vmem((2, 128, 1792), BF16), vmem((2, 1792, 1024), BF16),
-            vmem((2, 8, 128, 256), BF16), vmem((2, 256, 1024), BF16),
-            vmem((4, 8, 128, 128), BF16), vmem((28, 256, 128), BF16),
+            vmem((2, 128, 1792), BF16), vmem((3712, 1024), BF16),
+            vmem((2, 16, 256), BF16), vmem((2, 8, 2, 4, 16, 256), BF16),
+            vmem((256, 1024), BF16),
+            vmem((4, 8, 128, 128), BF16), vmem((8, 4, 256, 128), BF16),
             vmem((8, 256, 128), F32), vmem((4, 256, 128), BF16),
             vmem((4, 256, 128), BF16), vmem((4, 256, 128), BF16),
             vmem((8, 256, 128), BF16), vmem((8, 256, 128), BF16),
             vmem((256, 128), F32), vmem((2, 64, 128), F32),
             vmem((4, 256, 128), F32), vmem((256, 256), F32),
-            dma, dma, dma((16,)), dma((8,)), dma((8,)), dma((2, 8)), dma((32,)),
-            dma((4,)), dma((32,)), dma((28,)), dma((4,)), dma((4,)), dma((4,)),
+            dma, dma((2,)), dma((16,)), dma, dma((7,)), dma, dma((8,)), dma((2, 4)),
+            dma((8,)), dma((2,)), dma((32,)), dma((4,)), dma((12,)), dma((8, 4)),
+            dma((16,)), dma((4,)), dma((4,)), dma((4,)),
             dma((8,)), dma((8,)), dma((4,)), dma((8,)), dma((4,)), dma((2,)),
         ],
         compiler_params=pltpu.CompilerParams(

time: 80.1 us -> 71.3 us (0.89)
  Pallas kernels: 74.6 us -> 65.8 us
    pallas_call x1, Pallas kernels: 74.6 us -> 65.8 us  [body(): pl.pallas_call(kernel, out_shape=(jax.ShapeDtypeStruct((256, 1024), BF16)...]
where the time goes in v2:
time: 71.3 us; the launch traced here: 71.2 us
  Pallas kernels  65.8 us (92%)
  matrix products  2.95 us (4%)
  local copies, waits for them, and re-layouts  1.8 us (3%)
    pallas_call x1, Pallas kernels, body(): pl.pallas_call(kernel, out_shape=(jax.ShapeDtypeStruct((256, 1024), BF16)...  65.8 us
    dot_general x1, matrix products, body(): correction = jnp.dot(grams, answer, preferred_element_type=F32)  2.95 us
    unnamed x3, local copies, waits for them, and re-layouts  1.8 us

profile of v2, /device:TPU:1, one launch (start us, length us, event | category | flops | bytes accessed | tf_op | source)
XLA Modules:
  0.0 71.2 jit_solution(10133918454887129877)
XLA Ops:
  0.6 0.0 copy-start
  0.6 1.2 %copy-done = bf16[2,128,1792]{2,1,0:T(8,128)(2,1)S(1)} copy-done((bf16[2,128,1792]{2,1,0:T(8,128)(2,1)S(1)}, bf16[2,128,1792]{2,1,0:T(8,128)(2,1)}, u32[]{:S(2)}) %copy-start) | copy-done | bytes 917528
  1.8 65.8 %shard_map.41 = (bf16[256,1024]{1,0:T(8,128)(2,1)S(1)}, bf16[1792,256]{1,0:T(8,128)(2,1)S(1)}, f32[64,256]{1,0:T(8,128)S(1)}) custom-call(bf16[2,128,1792]{2,1,0:T(8,128)(2,1)S(1)} %copy-done, bf16[2,1792,1024]{2,1,0:T(8,128)(2,1)} %wts.1), custom_call_target="tpu_custom_call" | custom-call | tf_op jit(solution)/shard_map/pallas_call | solution.py:497
  67.6 3.0 %convolution_convert_fusion = bf16[1792,1024]{1,0:T(8,128)(2,1)} fusion(bf16[1792,256]{1,0:T(8,128)(2,1)S(1)} %get-tuple-element.6, bf16[256,1024]{1,0:T(8,128)(2,1)S(1)} %get-tuple-element.7), kind=kOutput, calls=%fused_computation | convolution fusion | flops 941359104 | bytes 5111808 | tf_op jit(solution)/shard_map/dot_general | solution.py:526
  70.5 0.6 copy.5
Async XLA Ops:
  0.6 1.2 %copy-start = (bf16[2,128,1792]{2,1,0:T(8,128)(2,1)S(1)}, bf16[2,128,1792]{2,1,0:T(8,128)(2,1)}, u32[]{:S(2)}) copy-start(bf16[2,128,1792]{2,1,0:T(8,128)(2,1)} %acts.1) | copy-start | bytes 2752516

commit v3 on v2

--- a/solution.py
+++ b/solution.py
@@ -63,9 +63,9 @@
 
 
 def kernel(
-    acts, wts, zout, smout, solout,
-    xv, wv, pa, pb, pt, xg, gt, rp, rsend, rin, r2, r2in, zb, solb, solin, big, sinv,
-    xsem, wsem, asend, arecv, bsend, brecv, csend, crecv, fsend, frecv,
+    acts, wts, corout, solout,
+    wv, pa, pb, pt, xg, gt, rp, rsend, rin, r2, r2in, zb, solb, solin, big, sinv, sm,
+    wsem, asend, arecv, bsend, brecv, csend, crecv, fsend, frecv,
     xsend, xrecv, gsend, grecv, hsend,
     dsend, drecv, rsems, rrecv, zsend, zfwd, zrecv, ssend, srecv,
 ):
@@ -90,8 +90,6 @@
     def arrived(ref, sem):
         pltpu.make_async_copy(ref, ref, sem).wait()
 
-    load_x = pltpu.make_async_copy(acts, xv, xsem)
-    load_x.start()
     load_w = [
         pltpu.make_async_copy(wts.at[m], wv.at[pl.ds(1792 * m, 1792), :], wsem.at[m])
         for m in range(2)
@@ -107,27 +105,35 @@
     for e in range(1, 16):
         dev = {"row": lax.rem(row + e // 4, 4), "col": lax.rem(col + e % 4, 4)}
         pl.semaphore_signal(barrier, inc=1, device_id=dev, device_id_type=MESH)
+    source = jnp.logical_and(row == 0, col == 0)
+
+    @pl.when(jnp.logical_not(source))
+    def _():
+        dev = {"tok": at(0, 1), "row": 0, "col": 0}
+        pl.semaphore_signal(barrier, inc=1, device_id=dev, device_id_type=MESH)
 
     wv[3584:, :] = jnp.zeros((128, 1024), BF16)
     for k in range(4):
         gt[2 * k + 1 - core, 3] = jnp.zeros((PANEL, 128), BF16)
-    load_x.wait()
-    pl.semaphore_wait(barrier, 22)
-
-    source = jnp.logical_and(row == 0, col == 0)
-
-    def scatter(e):
+    pl.semaphore_wait(barrier, jnp.where(source, 37, 22))
+
+    def scatter(dz, e):
         first = 16 * (e // 4 % 2 * 4 + e % 4)
-        return remote(
-            xv.at[:, first : first + 16, 0:PANEL], pa, asend.at[e], arecv,
-            {"row": e // 4, "col": e % 4},
+        dev = {"tok": at(0, dz), "row": e // 4, "col": e % 4}
+        return remote(
+            acts.at[:, first : first + 16, 0:PANEL], pa.at[zlo], asend.at[dz, e],
+            arecv.at[zlo], dev,
         )
 
     @pl.when(source)
     def _():
-        for e in (4, 1, 3, 5, 7, 8, 9, 11, 12, 13, 15, 2, 6, 10, 14):
-            scatter(e).start()
-        pa[...] = xv[:, 0:16, 0:PANEL]
+        for e in (2, 10, 6, 14, 1, 3, 9, 11, 5, 7, 13, 15, 8, 12, 0, 4):
+            for dz in (1, 0):
+                if dz or e:
+                    scatter(dz, e).start()
+        pltpu.make_async_copy(
+            acts.at[:, 0:16, 0:PANEL], pa.at[zlo], arecv.at[zlo]
+        ).start()
 
     offsets = ((1, 1), (3, 0), (0, 1), (3, 1), (1, 0), (2, 1), (2, 0))
 
@@ -140,7 +146,7 @@
                 acts.at[unit // 14, :, lanes], xg.at[slot, t], xrecv.at[slot]
             )
         return remote(
-            xv.at[unit // 14, :, lanes], xg.at[slot, t], xsend.at[slot * 8 + d],
+            acts.at[unit // 14, :, lanes], xg.at[slot, t], xsend.at[slot * 8 + d],
             xrecv.at[slot], {"tok": tt},
         )
 
@@ -162,48 +168,64 @@
             pa, pb.at[:, t, core, col], bsend.at[d], brecv, {"tok": at(*offsets[d])}
         )
 
-    @pl.when(jnp.logical_not(source))
-    def _():
-        arrived(pa, arecv)
-
-    for d in range(7):
-        spread(d).start()
-    pb[:, t, core, col] = pa[...]
+    def panel_of(k):
+        return lax.rem(zlo + k, 2)
+
+    def spread(k, d):
+        m = panel_of(k)
+        return remote(
+            pa.at[:, m], pb.at[m, :, x, core, col], bsend.at[k * 4 + d],
+            brecv.at[k, x], {"tok": at(d, 0)},
+        )
+
+    def along(k, b, d):
+        m = panel_of(k)
+        piece = pb.at[m, :, lax.rem(x + b, 4), core, col]
+        return remote(
+            piece, piece, csend.at[k * 16 + b * 4 + d], crecv.at[k, col],
+            {"col": lax.rem(col + d, 4)},
+        )
+
+    def across(k, d):
+        m = panel_of(k)
+        piece = pb.at[m, :, :, core, lax.rem(col + d, 4)]
+        return remote(piece, piece, fsend.at[k * 4 + d], frecv.at[k], partner)
+
+    for side in range(2):
+        arrived(pa.at[side], arecv.at[side])
+    for k in range(2):
+        for d in (2, 1, 3):
+            spread(k, d).start()
+        m = panel_of(k)
+        pb[m, :, x, core, col] = pa[:, m]
+        for d in (2, 1, 3):
+            along(k, 0, d).start()
     for slot in range(1, 4):
         send_slot(slot)
-    arrived(pb.at[:, 0:7, core, col], brecv)
-
-    def along(k, d):
-        m = lax.rem(zlo + k, 2)
-        piece = pb.at[m, :, core, col]
-        return remote(
-            piece, piece, csend.at[k * 4 + d], crecv.at[k, col],
-            {"col": lax.rem(col + d, 4)},
-        )
-
-    def across(k, d):
-        m = lax.rem(zlo + k, 2)
-        piece = pb.at[m, :, core, lax.rem(col + d, 4)]
-        return remote(piece, piece, fsend.at[k * 4 + d], frecv.at[k], partner)
-
-    for k in range(2):
-        for d in (1, 3, 2):
-            along(k, d).start()
-    for k in range(2):
+
+    def pass_on(k):
+        for b in (1, 3, 2):
+            other = lax.rem(x + b, 4)
+            m = panel_of(k)
+            arrived(pb.at[m, :, other, core, col], brecv.at[k, other])
+            for d in (2, 1, 3):
+                along(k, b, d).start()
         across(k, 0).start()
 
     def collect(k):
-        m = lax.rem(zlo + k, 2)
+        m = panel_of(k)
         for d in (1, 3, 2):
             other = lax.rem(col + d, 4)
-            arrived(pb.at[m, :, core, other], crecv.at[k, other])
+            arrived(pb.at[m, :, :, core, other], crecv.at[k, other])
             across(k, d).start()
 
     def whole_panel(k):
-        m = lax.rem(zlo + k, 2)
-        arrived(pb.at[m, :, 1 - core], frecv.at[k])
+        m = panel_of(k)
+        arrived(pb.at[m, :, :, 1 - core], frecv.at[k])
         return pb[m].reshape(1024, PANEL)
 
+    pass_on(0)
+    pass_on(1)
     collect(0)
     tokens = whole_panel(0)
     flipped = jnp.transpose(tokens)
@@ -299,7 +321,7 @@
             copy.start()
 
         when_there(across_z, slot, from_z)
-        when_there(relay_x(slot)[0], slot, from_x)
+        when_there(left if slot < 2 else right, slot, from_x)
 
     def forward_far(slot):
         def action():
@@ -332,57 +354,57 @@
     panels(8, 10)
     forward_far(3)
     take(right, (0, 1))
-    panels(10, 13)
+    panels(10, 11)
     accumulate(far)
+    take(at(1, 1))
+    take(at(3, 1))
+    take(at(2, 1))
+
+    def flip(c):
+        for slot in range(4):
+            def action(slot=slot):
+                both = gt[c, slot].astype(F32) + gt[c + 4, slot].astype(F32)
+                rows = pl.ds(pl.multiple_of((first_unit(c, core) + slot) * 128, 128), 128)
+                sm[rows, :] = jnp.transpose(both).astype(BF16)
+
+            when_there(c, slot, action)
+
+    def group(i, which):
+        return 2 * i + lax.rem(which + i, 2)
+
+    def dcopy(i):
+        return remote(rsend.at[i], rin.at[i], dsend.at[i], drecv.at[i], partner)
+
+    for d in (2, 1, 3, 0):
+        i = lax.rem(col + d, 4)
+        rsend[i] = rp[group(i, 1 - core)].astype(BF16)
+        dcopy(i).start()
+    panels(11, 13)
+    solver = lax.rem(col + zhi, 2) == core
+    chip = zhi * 4 + col
+    mine = 2 * col + zhi
+
+    def rcopy(i):
+        dev = {"row": 2 * lax.rem(core + i, 2) + core, "col": i}
+        return remote(r2.at[i], r2in.at[chip], rsems.at[i], rrecv.at[chip], dev)
+
+    def unless_mine(d, action):
+        if d:
+            action()
+        else:
+            pl.when(jnp.logical_not(solver))(action)
+
+    for d in (2, 1, 3, 0):
+        i = lax.rem(col + d, 4)
+        arrived(rin.at[i], drecv.at[i])
+        r2[i] = (rp[group(i, core)] + rin[i].astype(F32)).astype(BF16)
+        unless_mine(d, lambda i=i: rcopy(i).start())
     panels(13, 16)
     inverse = jnp.concatenate([big[2], big[3]], axis=1)
     sinv[...] = lax.dot_general(
         inverse, inverse, (((0,), (0,)), ((), ())), precision=HIGHEST,
         preferred_element_type=F32,
     )
-    take(at(1, 1))
-    take(at(3, 1))
-    take(at(2, 1))
-
-    def flip(c):
-        for slot in range(4):
-            def action(slot=slot):
-                both = gt[c, slot].astype(F32) + gt[c + 4, slot].astype(F32)
-                rows = pl.ds(pl.multiple_of((first_unit(c, core) + slot) * 128, 128), 128)
-                smout[rows, :] = jnp.transpose(both).astype(BF16)
-
-            when_there(c, slot, action)
-
-    def group(i, which):
-        return 2 * i + lax.rem(which + i, 2)
-
-    def dcopy(i):
-        return remote(rsend.at[i], rin.at[i], dsend.at[i], drecv.at[i], partner)
-
-    for i in range(4):
-        rsend[i] = rp[group(i, 1 - core)].astype(BF16)
-        dcopy(i).start()
-    flip(0)
-    solver = lax.rem(col + zhi, 2) == core
-    chip = zhi * 4 + col
-    mine = 2 * col + zhi
-
-    def mine_is(i):
-        return jnp.logical_and(solver, i == col)
-
-    def rcopy(i):
-        dev = {"row": 2 * lax.rem(core + i, 2) + core, "col": i}
-        return remote(r2.at[i], r2in.at[chip], rsems.at[i], rrecv.at[chip], dev)
-
-    for i in range(4):
-        arrived(rin.at[i], drecv.at[i])
-        r2[i] = (rp[group(i, core)] + rin[i].astype(F32)).astype(BF16)
-
-        @pl.when(jnp.logical_not(mine_is(i)))
-        def _():
-            rcopy(i).start()
-
-    flip(1)
 
     def zcopy(e):
         dev = {
@@ -405,7 +427,7 @@
             whole = whole + r2in[other].astype(F32)
         answer = jnp.dot(sinv[...], whole, precision=HIGHEST, preferred_element_type=F32)
         zb[mine] = answer.astype(BF16)
-        for e in range(1, 8):
+        for e in (6, 2, 5, 7, 1, 3, 4):
             zcopy(e).start()
         inverse = jnp.concatenate([big[2], big[3]], axis=1)
         solb[...] = jnp.dot(inverse, whole, precision=HIGHEST, preferred_element_type=F32)
@@ -418,26 +440,36 @@
             def _():
                 solin[zhi] = solb[64 * rr : 64 * rr + 64, :]
 
-    flip(2)
-    flip(3)
-
-    def zforward(i):
-        q = group(i, core)
-        return remote(zb.at[q], zb.at[q], zfwd.at[i], zrecv.at[q], partner)
-
-    for i in range(4):
-        q = group(i, core)
-
-        @pl.when(jnp.logical_not(mine_is(i)))
-        def _():
-            arrived(zb.at[q], zrecv.at[q])
-
-        zforward(i).start()
-    for i in range(4):
+    for c in range(4):
+        flip(c)
+
+    def zforward(d):
+        q = group(lax.rem(col + d, 4), core)
+        return remote(zb.at[q], zb.at[q], zfwd.at[d], zrecv.at[q], partner)
+
+    def pass_answer(d):
+        q = group(lax.rem(col + d, 4), core)
+        unless_mine(d, lambda: arrived(zb.at[q], zrecv.at[q]))
+        zforward(d).start()
+
+    def correct(d):
+        i = lax.rem(col + d, 4)
         q = group(i, 1 - core)
         arrived(zb.at[q], zrecv.at[q])
-    for q in range(8):
-        zout[:, 128 * q : 128 * q + 128] = zb[q]
+        both = jnp.concatenate([zb[2 * i], zb[2 * i + 1]], axis=1)
+        lanes = pl.ds(pl.multiple_of(256 * i, 256), 256)
+        corout[:, lanes] = jnp.dot(
+            sm[...], both, preferred_element_type=F32
+        ).astype(BF16)
+
+    pass_answer(0)
+    pass_answer(1)
+    pass_answer(3)
+    correct(0)
+    pass_answer(2)
+    correct(1)
+    correct(3)
+    correct(2)
     for h in range(2):
         @pl.when(jnp.logical_not(jnp.logical_and(solver, zhi == h)))
         def _():
@@ -447,11 +479,12 @@
 
     @pl.when(source)
     def _():
-        for e in range(1, 16):
-            scatter(e).wait_send()
+        for dz in range(2):
+            for e in range(16):
+                if dz or e:
+                    scatter(dz, e).wait_send()
 
     for d in range(7):
-        spread(d).wait_send()
         for slot in range(4):
             when_there(
                 at(*offsets[d]), slot, lambda slot=slot: xcopy(d, slot).wait_send()
@@ -460,7 +493,9 @@
         for d in range(4):
             across(k, d).wait_send()
             if d:
-                along(k, d).wait_send()
+                spread(k, d).wait_send()
+                for b in range(4):
+                    along(k, b, d).wait_send()
     for slot in range(4):
         def sent(slot=slot):
             for copy in own_sends(slot):
@@ -470,16 +505,15 @@
             relay_far(slot).wait_send()
 
         when_there(t, slot, sent)
-        tt, copy = relay_x(slot)
-        when_there(tt, slot, lambda copy=copy: copy.wait_send())
-
-    for i in range(4):
-        dcopy(i).wait_send()
-        zforward(i).wait_send()
-
-        @pl.when(jnp.logical_not(mine_is(i)))
-        def _():
-            rcopy(i).wait_send()
+        when_there(
+            left if slot < 2 else right, slot,
+            lambda slot=slot: relay_x(slot)[1].wait_send(),
+        )
+
+    for d in range(4):
+        dcopy(d).wait_send()
+        zforward(d).wait_send()
+        unless_mine(d, lambda: rcopy(lax.rem(col + d, 4)).wait_send())
 
     @pl.when(solver)
     def _():
@@ -497,34 +531,32 @@
     outs = pl.pallas_call(
         kernel,
         out_shape=(
-            jax.ShapeDtypeStruct((256, 1024), BF16),
-            jax.ShapeDtypeStruct((1792, 256), BF16),
+            jax.ShapeDtypeStruct((1792, 1024), BF16),
             jax.ShapeDtypeStruct((64, 256), F32),
         ),
-        in_specs=[pl.BlockSpec(memory_space=pl.ANY)] * 2,
-        out_specs=(pl.BlockSpec(memory_space=pltpu.VMEM),) * 3,
+        in_specs=[pl.BlockSpec(memory_space=pltpu.HBM)] * 2,
+        out_specs=(pl.BlockSpec(memory_space=pltpu.VMEM),) * 2,
         scratch_shapes=[
-            vmem((2, 128, 1792), BF16), vmem((3712, 1024), BF16),
-            vmem((2, 16, 256), BF16), vmem((2, 8, 2, 4, 16, 256), BF16),
+            vmem((3712, 1024), BF16),
+            vmem((2, 2, 16, 256), BF16), vmem((2, 2, 4, 2, 4, 16, 256), BF16),
             vmem((256, 1024), BF16),
             vmem((4, 8, 128, 128), BF16), vmem((8, 4, 256, 128), BF16),
             vmem((8, 256, 128), F32), vmem((4, 256, 128), BF16),
             vmem((4, 256, 128), BF16), vmem((4, 256, 128), BF16),
             vmem((8, 256, 128), BF16), vmem((8, 256, 128), BF16),
             vmem((256, 128), F32), vmem((2, 64, 128), F32),
-            vmem((4, 256, 128), F32), vmem((256, 256), F32),
-            dma, dma((2,)), dma((16,)), dma, dma((7,)), dma, dma((8,)), dma((2, 4)),
-            dma((8,)), dma((2,)), dma((32,)), dma((4,)), dma((12,)), dma((8, 4)),
+            vmem((4, 256, 128), F32), vmem((256, 256), F32), vmem((1792, 256), BF16),
+            dma((2,)), dma((2, 16)), dma((2,)), dma((8,)), dma((2, 4)), dma((32,)),
+            dma((2, 4)), dma((8,)), dma((2,)), dma((32,)), dma((4,)), dma((12,)), dma((8, 4)),
             dma((16,)), dma((4,)), dma((4,)), dma((4,)),
             dma((8,)), dma((8,)), dma((4,)), dma((8,)), dma((4,)), dma((2,)),
         ],
         compiler_params=pltpu.CompilerParams(
-            collective_id=0, has_side_effects=True, vmem_limit_bytes=48 * 1024 * 1024
+            collective_id=0, has_side_effects=True, vmem_limit_bytes=48_000_000
         ),
     )(activations, weights)
-    answer, grams, solved = outs
-    correction = jnp.dot(grams, answer, preferred_element_type=F32)
-    return solved, correction.astype(BF16)
+    correction, solved = outs
+    return solved, correction
 
 
 def solution(mesh):

time: 71.3 us -> 66 us (0.926)
  Pallas kernels: 65.8 us -> 61.6 us
  matrix products: 2.95 us -> 0 us
  local copies, waits for them, and re-layouts: 1.8 us -> 3.64 us
    pallas_call x1, Pallas kernels: 65.8 us -> 61.6 us  [body(): pl.pallas_call(kernel, out_shape=(jax.ShapeDtypeStruct((1792, 1024), BF16...]
    dot_general x1 -> x0, matrix products: 2.95 us -> none  [body(): correction = jnp.dot(grams, answer, preferred_element_type=F32)]
    unnamed x3 -> x4, local copies, waits for them, and re-layouts: 1.8 us -> 3.64 us
where the time goes in v3:
time: 66 us; the launch traced here: 65.9 us
  Pallas kernels  61.6 us (93%)
  local copies, waits for them, and re-layouts  3.64 us (6%)
    pallas_call x1, Pallas kernels, body(): pl.pallas_call(kernel, out_shape=(jax.ShapeDtypeStruct((1792, 1024), BF16...  61.6 us
    unnamed x4, local copies, waits for them, and re-layouts  3.64 us

profile of v3, /device:TPU:1, one launch (start us, length us, event | category | flops | bytes accessed | tf_op | source)
XLA Modules:
  0.0 65.9 jit_solution(11175646232023354296)
XLA Ops:
  0.6 0.0 copy-start
  0.6 1.2 %copy-done = bf16[2,128,1792]{2,1,0:T(8,128)(2,1)S(1)} copy-done((bf16[2,128,1792]{2,1,0:T(8,128)(2,1)S(1)}, bf16[2,128,1792]{2,1,0:T(8,128)(2,1)}, u32[]{:S(2)}) %copy-start) | copy-done | bytes 917528
  1.8 61.6 %shard_map.41 = (bf16[1792,1024]{1,0:T(8,128)(2,1)S(1)}, f32[64,256]{1,0:T(8,128)S(1)}) custom-call(bf16[2,128,1792]{2,1,0:T(8,128)(2,1)S(1)} %copy-done, bf16[2,1792,1024]{2,1,0:T(8,128)(2,1)} %wts.1), custom_call_target="tpu_custom_call" | custom-call | tf_op jit(solution)/shard_map/pallas_call | solution.py:531
  63.4 0.6 copy.6
  64.1 1.8 %copy.7 = bf16[1792,1024]{1,0:T(8,128)(2,1)} copy(bf16[1792,1024]{1,0:T(8,128)(2,1)S(1)} %get-tuple-element.9) | data formatting | bytes 7340032
Async XLA Ops:
  0.6 1.2 %copy-start = (bf16[2,128,1792]{2,1,0:T(8,128)(2,1)S(1)}, bf16[2,128,1792]{2,1,0:T(8,128)(2,1)}, u32[]{:S(2)}) copy-start(bf16[2,128,1792]{2,1,0:T(8,128)(2,1)} %acts.1) | copy-start | bytes 2752516

commit v4 on v3

--- a/solution.py
+++ b/solution.py
@@ -64,10 +64,10 @@
 
 def kernel(
     acts, wts, corout, solout,
-    wv, pa, pb, pt, xg, gt, rp, rsend, rin, r2, r2in, zb, solb, solin, big, sinv, sm,
-    wsem, asend, arecv, bsend, brecv, csend, crecv, fsend, frecv,
+    xv, wv, pa, pb, pt, xg, gt, rp, rsend, rin, r2, r2in, zb, big, sm,
+    xsem, wsem, asend, arecv, bsend, brecv, csend, crecv, fsend, frecv,
     xsend, xrecv, gsend, grecv, hsend,
-    dsend, drecv, rsems, rrecv, zsend, zfwd, zrecv, ssend, srecv,
+    dsend, drecv, rsems, rrecv, zsend, zfwd, zrecv,
 ):
     t = lax.axis_index("tok")
     row = lax.axis_index("row")
@@ -90,6 +90,8 @@
     def arrived(ref, sem):
         pltpu.make_async_copy(ref, ref, sem).wait()
 
+    load_x = pltpu.make_async_copy(acts, xv, xsem)
+    load_x.start()
     load_w = [
         pltpu.make_async_copy(wts.at[m], wv.at[pl.ds(1792 * m, 1792), :], wsem.at[m])
         for m in range(2)
@@ -102,38 +104,40 @@
         pl.semaphore_signal(
             barrier, inc=1, device_id={"tok": lax.rem(t + d, 8)}, device_id_type=MESH
         )
-    for e in range(1, 16):
-        dev = {"row": lax.rem(row + e // 4, 4), "col": lax.rem(col + e % 4, 4)}
-        pl.semaphore_signal(barrier, inc=1, device_id=dev, device_id_type=MESH)
     source = jnp.logical_and(row == 0, col == 0)
 
     @pl.when(jnp.logical_not(source))
     def _():
-        dev = {"tok": at(0, 1), "row": 0, "col": 0}
-        pl.semaphore_signal(barrier, inc=1, device_id=dev, device_id_type=MESH)
+        for dz in range(2):
+            dev = {"tok": at(0, dz), "row": 0, "col": 0}
+            pl.semaphore_signal(barrier, inc=1, device_id=dev, device_id_type=MESH)
 
     wv[3584:, :] = jnp.zeros((128, 1024), BF16)
     for k in range(4):
         gt[2 * k + 1 - core, 3] = jnp.zeros((PANEL, 128), BF16)
-    pl.semaphore_wait(barrier, jnp.where(source, 37, 22))
-
-    def scatter(dz, e):
+    load_x.wait()
+    pl.semaphore_wait(barrier, jnp.where(source, 37, 7))
+
+    def scatter(k, dz, e):
         first = 16 * (e // 4 % 2 * 4 + e % 4)
+        m = lax.rem(zlo + dz + k, 2)
         dev = {"tok": at(0, dz), "row": e // 4, "col": e % 4}
         return remote(
-            acts.at[:, first : first + 16, 0:PANEL], pa.at[zlo], asend.at[dz, e],
-            arecv.at[zlo], dev,
+            xv.at[m, first : first + 16, 0:PANEL], pa.at[zlo, m], asend.at[k, dz, e],
+            arecv.at[zlo, k], dev,
         )
 
     @pl.when(source)
     def _():
-        for e in (2, 10, 6, 14, 1, 3, 9, 11, 5, 7, 13, 15, 8, 12, 0, 4):
-            for dz in (1, 0):
-                if dz or e:
-                    scatter(dz, e).start()
-        pltpu.make_async_copy(
-            acts.at[:, 0:16, 0:PANEL], pa.at[zlo], arecv.at[zlo]
-        ).start()
+        for k in range(2):
+            for e in (2, 10, 6, 14, 1, 3, 9, 11, 5, 7, 13, 15, 8, 12, 0, 4):
+                for dz in (1, 0):
+                    if dz or e:
+                        scatter(k, dz, e).start()
+            m = lax.rem(zlo + k, 2)
+            pltpu.make_async_copy(
+                acts.at[m, 0:16, 0:PANEL], pa.at[zlo, m], arecv.at[zlo, k]
+            ).start()
 
     offsets = ((1, 1), (3, 0), (0, 1), (3, 1), (1, 0), (2, 1), (2, 0))
 
@@ -146,7 +150,7 @@
                 acts.at[unit // 14, :, lanes], xg.at[slot, t], xrecv.at[slot]
             )
         return remote(
-            acts.at[unit // 14, :, lanes], xg.at[slot, t], xsend.at[slot * 8 + d],
+            xv.at[unit // 14, :, lanes], xg.at[slot, t], xsend.at[slot * 8 + d],
             xrecv.at[slot], {"tok": tt},
         )
 
@@ -191,17 +195,21 @@
         piece = pb.at[m, :, :, core, lax.rem(col + d, 4)]
         return remote(piece, piece, fsend.at[k * 4 + d], frecv.at[k], partner)
 
-    for side in range(2):
-        arrived(pa.at[side], arecv.at[side])
-    for k in range(2):
+    def enter(k):
+        m = panel_of(k)
+        for side in range(2):
+            arrived(pa.at[side, m], arecv.at[side, k])
         for d in (2, 1, 3):
             spread(k, d).start()
-        m = panel_of(k)
         pb[m, :, x, core, col] = pa[:, m]
         for d in (2, 1, 3):
             along(k, 0, d).start()
-    for slot in range(1, 4):
-        send_slot(slot)
+
+    enter(0)
+    send_slot(1)
+    enter(1)
+    send_slot(2)
+    send_slot(3)
 
     def pass_on(k):
         for b in (1, 3, 2):
@@ -334,6 +342,15 @@
         for slot in slots:
             when_there(tt, slot, lambda slot=slot: unit_in(tt, slot))
         accumulate(tt)
+
+    def flip(c):
+        for slot in range(4):
+            def action(slot=slot):
+                both = gt[c, slot].astype(F32) + gt[c + 4, slot].astype(F32)
+                rows = pl.ds(pl.multiple_of((first_unit(c, core) + slot) * 128, 128), 128)
+                sm[rows, :] = jnp.transpose(both).astype(BF16)
+
+            when_there(c, slot, action)
 
     for load in load_w:
         load.wait()
@@ -356,18 +373,10 @@
     take(right, (0, 1))
     panels(10, 11)
     accumulate(far)
+    flip(x)
     take(at(1, 1))
     take(at(3, 1))
     take(at(2, 1))
-
-    def flip(c):
-        for slot in range(4):
-            def action(slot=slot):
-                both = gt[c, slot].astype(F32) + gt[c + 4, slot].astype(F32)
-                rows = pl.ds(pl.multiple_of((first_unit(c, core) + slot) * 128, 128), 128)
-                sm[rows, :] = jnp.transpose(both).astype(BF16)
-
-            when_there(c, slot, action)
 
     def group(i, which):
         return 2 * i + lax.rem(which + i, 2)
@@ -400,23 +409,14 @@
         r2[i] = (rp[group(i, core)] + rin[i].astype(F32)).astype(BF16)
         unless_mine(d, lambda i=i: rcopy(i).start())
     panels(13, 16)
-    inverse = jnp.concatenate([big[2], big[3]], axis=1)
-    sinv[...] = lax.dot_general(
-        inverse, inverse, (((0,), (0,)), ((), ())), precision=HIGHEST,
-        preferred_element_type=F32,
-    )
+    for b in range(1, 4):
+        flip(lax.rem(x + b, 4))
 
     def zcopy(e):
         dev = {
             "row": 2 * lax.rem(zhi + e // 4, 2) + core, "col": lax.rem(col + e % 4, 4)
         }
         return remote(zb.at[mine], zb.at[mine], zsend.at[e], zrecv.at[mine], dev)
-
-    def scopy(rr):
-        return remote(
-            solb.at[pl.ds(64 * rr, 64), :], solin.at[zhi], ssend.at[rr], srecv.at[zhi],
-            {"row": rr, "col": col},
-        )
 
     @pl.when(solver)
     def _():
@@ -425,23 +425,21 @@
             other = lax.rem(chip + e, 8)
             arrived(r2in.at[other], rrecv.at[other])
             whole = whole + r2in[other].astype(F32)
-        answer = jnp.dot(sinv[...], whole, precision=HIGHEST, preferred_element_type=F32)
-        zb[mine] = answer.astype(BF16)
+        zb[mine] = whole.astype(BF16)
         for e in (6, 2, 5, 7, 1, 3, 4):
             zcopy(e).start()
-        inverse = jnp.concatenate([big[2], big[3]], axis=1)
-        solb[...] = jnp.dot(inverse, whole, precision=HIGHEST, preferred_element_type=F32)
-        for rr in range(4):
-            @pl.when(rr != row)
-            def _():
-                scopy(rr).start()
-
-            @pl.when(rr == row)
-            def _():
-                solin[zhi] = solb[64 * rr : 64 * rr + 64, :]
-
-    for c in range(4):
-        flip(c)
+
+    inverse = jnp.concatenate([big[2], big[3]], axis=1)
+    both_sides = lax.dot_general(
+        inverse, inverse, (((0,), (0,)), ((), ())), precision=HIGHEST,
+        preferred_element_type=F32,
+    )
+    sh, sl, _ = split3(both_sides)
+    halves = jnp.concatenate([sh, sl], axis=1)
+    for k in range(7):
+        rows = slice(256 * k, 256 * k + 256)
+        pair = jnp.dot(sm[rows, :], halves, preferred_element_type=F32)
+        sm[rows, :] = (pair[:, :PANEL] + pair[:, PANEL:]).astype(BF16)
 
     def zforward(d):
         q = group(lax.rem(col + d, 4), core)
@@ -466,23 +464,24 @@
     pass_answer(1)
     pass_answer(3)
     correct(0)
+    these = pl.ds(pl.multiple_of(64 * row, 64), 64)
+    right_side = jnp.concatenate([zb[2 * col], zb[2 * col + 1]], axis=1)
+    solout[...] = jnp.dot(
+        jnp.concatenate([big[2, these, :], big[3, these, :]], axis=1),
+        right_side.astype(F32), precision=HIGHEST, preferred_element_type=F32,
+    )
     pass_answer(2)
     correct(1)
     correct(3)
     correct(2)
-    for h in range(2):
-        @pl.when(jnp.logical_not(jnp.logical_and(solver, zhi == h)))
-        def _():
-            arrived(solin.at[h], srecv.at[h])
-
-        solout[:, 128 * h : 128 * h + 128] = solin[h]
 
     @pl.when(source)
     def _():
-        for dz in range(2):
-            for e in range(16):
-                if dz or e:
-                    scatter(dz, e).wait_send()
+        for k in range(2):
+            for dz in range(2):
+                for e in range(16):
+                    if dz or e:
+                        scatter(k, dz, e).wait_send()
 
     for d in range(7):
         for slot in range(4):
@@ -519,10 +518,6 @@
     def _():
         for e in range(1, 8):
             zcopy(e).wait_send()
-        for rr in range(4):
-            @pl.when(rr != row)
-            def _():
-                scopy(rr).wait_send()
 
 
 def body(activations, weights):
@@ -537,24 +532,23 @@
         in_specs=[pl.BlockSpec(memory_space=pltpu.HBM)] * 2,
         out_specs=(pl.BlockSpec(memory_space=pltpu.VMEM),) * 2,
         scratch_shapes=[
-            vmem((3712, 1024), BF16),
+            vmem((2, 128, 1792), BF16), vmem((3712, 1024), BF16),
             vmem((2, 2, 16, 256), BF16), vmem((2, 2, 4, 2, 4, 16, 256), BF16),
             vmem((256, 1024), BF16),
             vmem((4, 8, 128, 128), BF16), vmem((8, 4, 256, 128), BF16),
             vmem((8, 256, 128), F32), vmem((4, 256, 128), BF16),
             vmem((4, 256, 128), BF16), vmem((4, 256, 128), BF16),
             vmem((8, 256, 128), BF16), vmem((8, 256, 128), BF16),
-            vmem((256, 128), F32), vmem((2, 64, 128), F32),
-            vmem((4, 256, 128), F32), vmem((256, 256), F32), vmem((1792, 256), BF16),
-            dma((2,)), dma((2, 16)), dma((2,)), dma((8,)), dma((2, 4)), dma((32,)),
+            vmem((4, 256, 128), F32), vmem((1792, 256), BF16),
+            dma, dma((2,)), dma((2, 2, 16)), dma((2, 2)), dma((8,)), dma((2, 4)), dma((32,)),
             dma((2, 4)), dma((8,)), dma((2,)), dma((32,)), dma((4,)), dma((12,)), dma((8, 4)),
             dma((16,)), dma((4,)), dma((4,)), dma((4,)),
-            dma((8,)), dma((8,)), dma((4,)), dma((8,)), dma((4,)), dma((2,)),
+            dma((8,)), dma((8,)), dma((4,)), dma((8,)),
         ],
         compiler_params=pltpu.CompilerParams(
             collective_id=0, has_side_effects=True, vmem_limit_bytes=48_000_000
         ),
-    )(activations, weights)
+    )(pltpu.with_memory_space_constraint(activations, pltpu.HBM), weights)
     correction, solved = outs
     return solved, correction
 

time: 66 us -> 63.7 us (0.965)
  Pallas kernels: 61.6 us -> 60.4 us
  local copies, waits for them, and re-layouts: 3.64 us -> 2.47 us
    pallas_call x1, Pallas kernels: 61.6 us -> 60.4 us  [body(): pl.pallas_call(kernel, out_shape=(jax.ShapeDtypeStruct((1792, 1024), BF16...]
    unnamed x4 -> x2, local copies, waits for them, and re-layouts: 3.64 us -> 2.47 us
where the time goes in v4:
time: 63.7 us; the launch traced here: 63.5 us
  Pallas kernels  60.4 us (95%)
  local copies, waits for them, and re-layouts  2.47 us (4%)
  between operations  0.64 us (1%)
    pallas_call x1, Pallas kernels, body(): pl.pallas_call(kernel, out_shape=(jax.ShapeDtypeStruct((1792, 1024), BF16...  60.4 us
    unnamed x2, local copies, waits for them, and re-layouts  2.47 us

profile of v4, /device:TPU:1, one launch (start us, length us, event | category | flops | bytes accessed | tf_op | source)
XLA Modules:
  0.0 63.5 jit_solution(1895680567188912375)
XLA Ops:
  0.6 60.4 %shard_map.41 = (bf16[1792,1024]{1,0:T(8,128)(2,1)S(1)}, f32[64,256]{1,0:T(8,128)S(1)}) custom-call(bf16[2,128,1792]{2,1,0:T(8,128)(2,1)} %acts.1, bf16[2,1792,1024]{2,1,0:T(8,128)(2,1)} %wts.1), custom_call_target="tpu_custom_call" | custom-call | tf_op jit(solution)/shard_map/pallas_call | solution.py:526
  61.0 0.6 copy.6
  61.7 1.8 %copy.7 = bf16[1792,1024]{1,0:T(8,128)(2,1)} copy(bf16[1792,1024]{1,0:T(8,128)(2,1)S(1)} %get-tuple-element.9) | data formatting | bytes 7340032

commit v5 on v4

--- a/solution.py
+++ b/solution.py
@@ -348,7 +348,7 @@
             def action(slot=slot):
                 both = gt[c, slot].astype(F32) + gt[c + 4, slot].astype(F32)
                 rows = pl.ds(pl.multiple_of((first_unit(c, core) + slot) * 128, 128), 128)
-                sm[rows, :] = jnp.transpose(both).astype(BF16)
+                sm[rows, :] = jnp.transpose(both.astype(BF16))
 
             when_there(c, slot, action)
 
@@ -371,9 +371,10 @@
     panels(8, 10)
     forward_far(3)
     take(right, (0, 1))
-    panels(10, 11)
+    panels(10, 12)
     accumulate(far)
     flip(x)
+    panels(12, 14)
     take(at(1, 1))
     take(at(3, 1))
     take(at(2, 1))
@@ -388,7 +389,7 @@
         i = lax.rem(col + d, 4)
         rsend[i] = rp[group(i, 1 - core)].astype(BF16)
         dcopy(i).start()
-    panels(11, 13)
+    panels(14, 16)
     solver = lax.rem(col + zhi, 2) == core
     chip = zhi * 4 + col
     mine = 2 * col + zhi
@@ -408,7 +409,6 @@
         arrived(rin.at[i], drecv.at[i])
         r2[i] = (rp[group(i, core)] + rin[i].astype(F32)).astype(BF16)
         unless_mine(d, lambda i=i: rcopy(i).start())
-    panels(13, 16)
     for b in range(1, 4):
         flip(lax.rem(x + b, 4))
 
@@ -426,7 +426,7 @@
             arrived(r2in.at[other], rrecv.at[other])
             whole = whole + r2in[other].astype(F32)
         zb[mine] = whole.astype(BF16)
-        for e in (6, 2, 5, 7, 1, 3, 4):
+        for e in (6, 5, 7, 4, 2, 1, 3):
             zcopy(e).start()
 
     inverse = jnp.concatenate([big[2], big[3]], axis=1)
@@ -464,13 +464,13 @@
     pass_answer(1)
     pass_answer(3)
     correct(0)
+    pass_answer(2)
     these = pl.ds(pl.multiple_of(64 * row, 64), 64)
     right_side = jnp.concatenate([zb[2 * col], zb[2 * col + 1]], axis=1)
     solout[...] = jnp.dot(
         jnp.concatenate([big[2, these, :], big[3, these, :]], axis=1),
         right_side.astype(F32), precision=HIGHEST, preferred_element_type=F32,
     )
-    pass_answer(2)
     correct(1)
     correct(3)
     correct(2)

time: 63.7 us -> 63.3 us (level)
  no operation moved by 1% of the time
where the time goes in v5:
time: 63.3 us; the launch traced here: 63.1 us
  Pallas kernels  60 us (95%)
  local copies, waits for them, and re-layouts  2.47 us (4%)
  between operations  0.64 us (1%)
    pallas_call x1, Pallas kernels, body(): pl.pallas_call(kernel, out_shape=(jax.ShapeDtypeStruct((1792, 1024), BF16...  60 us
    unnamed x2, local copies, waits for them, and re-layouts  2.47 us

profile of v5, /device:TPU:1, one launch (start us, length us, event | category | flops | bytes accessed | tf_op | source)
XLA Modules:
  0.0 63.1 jit_solution(8254412949514391855)
XLA Ops:
  0.6 60.0 %shard_map.41 = (bf16[1792,1024]{1,0:T(8,128)(2,1)S(1)}, f32[64,256]{1,0:T(8,128)S(1)}) custom-call(bf16[2,128,1792]{2,1,0:T(8,128)(2,1)} %acts.1, bf16[2,1792,1024]{2,1,0:T(8,128)(2,1)} %wts.1), custom_call_target="tpu_custom_call" | custom-call | tf_op jit(solution)/shard_map/pallas_call | solution.py:526
  60.7 0.6 %copy.6 = f32[64,256]{1,0:T(8,128)} copy(f32[64,256]{1,0:T(8,128)S(1)} %get-tuple-element.8) | data formatting | bytes 131072
  61.3 1.8 %copy.7 = bf16[1792,1024]{1,0:T(8,128)(2,1)} copy(bf16[1792,1024]{1,0:T(8,128)(2,1)S(1)} %get-tuple-element.9) | data formatting | bytes 7340032

commit v6 on v5

--- a/solution.py
+++ b/solution.py
@@ -412,6 +412,10 @@
     for b in range(1, 4):
         flip(lax.rem(x + b, 4))
 
+    def zforward(d):
+        q = group(lax.rem(col + d, 4), core)
+        return remote(zb.at[q], zb.at[q], zfwd.at[d], zrecv.at[q], partner)
+
     def zcopy(e):
         dev = {
             "row": 2 * lax.rem(zhi + e // 4, 2) + core, "col": lax.rem(col + e % 4, 4)
@@ -428,6 +432,7 @@
         zb[mine] = whole.astype(BF16)
         for e in (6, 5, 7, 4, 2, 1, 3):
             zcopy(e).start()
+        zforward(0).start()
 
     inverse = jnp.concatenate([big[2], big[3]], axis=1)
     both_sides = lax.dot_general(
@@ -441,14 +446,14 @@
         pair = jnp.dot(sm[rows, :], halves, preferred_element_type=F32)
         sm[rows, :] = (pair[:, :PANEL] + pair[:, PANEL:]).astype(BF16)
 
-    def zforward(d):
-        q = group(lax.rem(col + d, 4), core)
-        return remote(zb.at[q], zb.at[q], zfwd.at[d], zrecv.at[q], partner)
-
     def pass_answer(d):
         q = group(lax.rem(col + d, 4), core)
-        unless_mine(d, lambda: arrived(zb.at[q], zrecv.at[q]))
-        zforward(d).start()
+
+        def pass_on_sum():
+            arrived(zb.at[q], zrecv.at[q])
+            zforward(d).start()
+
+        unless_mine(d, pass_on_sum)
 
     def correct(d):
         i = lax.rem(col + d, 4)
@@ -460,9 +465,9 @@
             sm[...], both, preferred_element_type=F32
         ).astype(BF16)
 
-    pass_answer(0)
     pass_answer(1)
     pass_answer(3)
+    pass_answer(0)
     correct(0)
     pass_answer(2)
     these = pl.ds(pl.multiple_of(64 * row, 64), 64)

time: 63.3 us -> 64.2 us (1.014); the launches traced: 63.1 us -> 63.1 us
  no operation moved by 1% of the time
where the time goes in v6:
time: 64.2 us; the launch traced here: 63.1 us
  Pallas kernels  60 us (93%)
  local copies, waits for them, and re-layouts  2.47 us (4%)
    pallas_call x1, Pallas kernels, body(): pl.pallas_call(kernel, out_shape=(jax.ShapeDtypeStruct((1792, 1024), BF16...  60 us
    unnamed x2, local copies, waits for them, and re-layouts  2.47 us

profile of v6, /device:TPU:1, one launch (start us, length us, event | category | flops | bytes accessed | tf_op | source)
XLA Modules:
  0.0 63.1 jit_solution(2425410556582599561)
XLA Ops:
  0.6 60.0 %shard_map.41 = (bf16[1792,1024]{1,0:T(8,128)(2,1)S(1)}, f32[64,256]{1,0:T(8,128)S(1)}) custom-call(bf16[2,128,1792]{2,1,0:T(8,128)(2,1)} %acts.1, bf16[2,1792,1024]{2,1,0:T(8,128)(2,1)} %wts.1), custom_call_target="tpu_custom_call" | custom-call | tf_op jit(solution)/shard_map/pallas_call | solution.py:531
  60.7 0.6 %copy.6 = f32[64,256]{1,0:T(8,128)} copy(f32[64,256]{1,0:T(8,128)S(1)} %get-tuple-element.8) | data formatting | bytes 131072
  61.3 1.8 %copy.7 = bf16[1792,1024]{1,0:T(8,128)(2,1)} copy(bf16[1792,1024]{1,0:T(8,128)(2,1)S(1)} %get-tuple-element.9) | data formatting | bytes 7340032
